TPU v7x, 256 devices: a whole 4x4x8 slice. The times are simulated.
256 devices in a mesh: dp: 16 (over z, x_hi), tensor: 16 (over y, x_lo, core).
Axes of the slice: x: 4 (x_hi: 2, x_lo: 2; x = x_hi * 2 + x_lo), y: 4, z: 8, core: 2. Of those that a mesh axis runs over, the one named last changes fastest.
Arguments:
- tokens: bfloat16 [16, 1024, 4096], P('dp', 'tensor'), may hold values from -6 to 6
- gain: bfloat16 [4096], replicated, may hold values from 0.5 to 1.5
- wq: bfloat16 [4096, 4096], P(None, 'tensor'), may hold values from -0.09375 to 0.09375
- bq: bfloat16 [4096], P('tensor'), may hold values from -5 to 5
- wkv: bfloat16 [4096, 1024], P(None, 'tensor'), may hold values from -0.09375 to 0.09375
- bkv: bfloat16 [1024], P('tensor'), may hold values from -5 to 5
- wo: bfloat16 [4096, 4096], P('tensor'), may hold values from -0.375 to 0.375
- check_weights: float32 [16, 1024], P('dp'), may hold values from -12 to 12
Outputs:
- attended: bfloat16 [16, 1024, 4096], P('dp', 'tensor')
- checksum: float32 [4096], replicated
All inputs are finite; a program needn't handle non-finite values.
Results may differ from a plain program's by a relative error of at most 0.018.
Values may be sent and summed in bfloat16 or wider, within the bound.
A program may use at most 64 MiB of HBM per device.

v0:
```python
import jax
import jax.numpy as jnp
from jax import lax
from jax.sharding import Mesh
from jax.sharding import PartitionSpec as P

HEADS = 32
KV = 4
HD = 128
TENSOR = ("tensor_0", "tensor_1", "tensor_2")
DP_TENSOR = ("dp_0", "dp_1", "tensor_0", "tensor_1", "tensor_2")
DP = ("dp_0", "dp_1")


EPS = 1e-06
THETA = 1000000.0


def sent_to_all(shard, axis):
    count = lax.axis_size(axis)
    return lax.all_to_all(
        jnp.broadcast_to(shard[None], (count, *shard.shape)), axis, 0, 0, tiled=True
    )


def in_order(pieces, dim):
    pieces = jnp.moveaxis(pieces, 0, dim)
    shape = pieces.shape
    return pieces.reshape(*shape[:dim], shape[dim] * shape[dim + 1], *shape[dim + 2 :])


def gather_directly(shard, axis, dim):
    pieces = sent_to_all(shard, axis)
    return in_order(pieces, dim)


def one_axis_at_a_time(shard, axes):
    for axis in axes:
        shard = lax.psum(shard, axis)
    return shard


def rope(values, head_size):
    rows = values.shape[0]
    half = head_size // 2
    inverse = THETA ** (-(jnp.arange(half, dtype=jnp.float32) * 2.0 / head_size))
    angles = jnp.arange(rows, dtype=jnp.float32)[:, None] * inverse[None, :]
    cosine = jnp.cos(angles)[:, None, :]
    sine = jnp.sin(angles)[:, None, :]
    shaped = values.reshape(rows, -1, head_size)
    first = shaped[..., :half]
    second = shaped[..., half:]
    turned = jnp.concatenate(
        [first * cosine - second * sine, second * cosine + first * sine], axis=-1
    )
    return turned.reshape(rows, -1)


def local(tokens, gain, wq, bq, wkv, bkv, wo, check_weights):
    states = tokens[0].astype(jnp.float32)
    normed = (
        states
        * lax.rsqrt(jnp.mean(states * states, axis=-1, keepdims=True) + EPS)
        * gain.astype(jnp.float32)
    ).astype(jnp.bfloat16)
    position = lax.axis_index(TENSOR)
    head_dev = wq.shape[1] // HD
    query_cols = head_dev * HD
    shared = position * head_dev // (HEADS // KV)
    joined_w = jnp.concatenate([wq, wkv], axis=1)
    joined_b = jnp.concatenate([bq, bkv], axis=0).astype(jnp.float32)
    projected = (
        jnp.dot(
            lax.all_gather(normed, TENSOR, axis=0, tiled=True),
            joined_w,
            preferred_element_type=jnp.float32,
        )
        + joined_b[None, :]
    )
    seq_rows = projected.shape[0]
    query = rope(projected[:, :query_cols], HD).astype(jnp.bfloat16)
    kv_local = projected[:, query_cols:].astype(jnp.bfloat16)
    kv_whole = gather_directly(kv_local, TENSOR, 1)
    key_part = lax.dynamic_slice_in_dim(kv_whole, shared * HD, HD, 1)
    values = lax.dynamic_slice_in_dim(kv_whole, KV * HD + shared * HD, HD, 1)
    keys = rope(key_part.astype(jnp.float32), HD).astype(jnp.bfloat16)
    scale = HD ** (-0.5)
    block = min(512, seq_rows)
    query_heads = query.reshape(seq_rows, head_dev, HD)
    pieces = []
    for number in range(seq_rows // block):
        stop = (number + 1) * block
        query_block = query_heads[number * block : stop]
        scores = (
            jnp.einsum("qhd,kd->hqk", query_block, keys[:stop], preferred_element_type=jnp.float32)
            * scale
        )
        allowed = jnp.arange(block)[:, None] + number * block >= jnp.arange(stop)[None, :]
        scores = jnp.where(allowed[None, :, :], scores, -1e30)
        probs = jax.nn.softmax(scores, axis=-1).astype(jnp.bfloat16)
        mixed = jnp.einsum(
            "hqk,kd->qhd", probs, values[:stop], preferred_element_type=jnp.float32
        ).astype(jnp.bfloat16)
        pieces.append(mixed.reshape(block, query_cols))
    context = jnp.concatenate(pieces, axis=0)
    summed = lax.psum_scatter(
        jnp.dot(context, wo, preferred_element_type=jnp.float32).astype(jnp.bfloat16),
        TENSOR,
        scatter_dimension=0,
        tiled=True,
    )
    attended = summed[None, :, :]
    summary = jnp.dot(
        check_weights[0], context.astype(jnp.float32), precision=lax.Precision.HIGHEST
    )
    term = jnp.dot(summary, wo.astype(jnp.float32), precision=lax.Precision.HIGHEST)
    total = one_axis_at_a_time(term, DP_TENSOR)
    checksum = total / jnp.sqrt(jnp.float32(seq_rows * lax.axis_size(DP)))
    return (attended, checksum)


def solution(mesh):
    torus = Mesh(
        mesh.devices.reshape(8, 2, 4, 2, 2), ("dp_0", "dp_1", "tensor_0", "tensor_1", "tensor_2")
    )
    return jax.shard_map(
        local,
        mesh=torus,
        in_specs=(
            P(DP, TENSOR, None),
            P(),
            P(None, TENSOR),
            P(TENSOR),
            P(None, TENSOR),
            P(TENSOR),
            P(TENSOR, None),
            P(DP, None),
        ),
        out_specs=(P(DP, TENSOR, None), P()),
        check_vma=False,
    )
```

profile of v0, /device:TPU:1, one launch (start us, length us, event | category | flops | bytes accessed | tf_op | source)
XLA Modules:
  0.0 239.8 jit_solution(9713088401268908276)
XLA Ops:
  7.2 0.0 copy-start
  7.2 0.0 copy-start.1
  7.2 0.0 copy-start.8
  7.2 0.0 copy-start.7
  7.2 0.0 all-gather.2.cloned.1.call-start
  7.3 0.9 convert_element_type.54
  8.1 1.2 fusion.16
  9.4 2.0 fusion.18
  11.4 0.0 all-gather.2.cloned.1.call-update
  11.4 0.0 copy-done.1
  11.4 1.4 copy.18
  12.8 0.0 copy-done.8
  12.9 0.0 copy-done.7
  12.9 57.5 %all-gather.2.cloned.1.call-done = bf16[1024,4096]{1,0:T(8,128)(2,1)} async-done(((bf16[64,4096]{1,0:T(8,128)(2,1)}), bf16[1024,4096]{1,0:T(8,128)(2,1)}) %all-gather.2.cloned.1.call-update) | async-done | bytes 8388624 | tf_op jit(solution)/shard_map/all_gather | solution.py:74
  70.4 7.2 %fusion.12 = f32[1024,320]{0,1:T(8,128)S(1)} fusion(bf16[1024,4096]{1,0:T(8,128)(2,1)} %all-gather.2.cloned.1.call-done, bf16[4096,64]{1,0:T(8,128)(2,1)} %copy.18, bf16[4096,256]{1,0:T(8,128)(2,1)} %param.10, f32[320]{0:T(512)S(1)} %maximum_convert_fusion), kind=kOutput, calls=%fused_computation.22 | convolution fusion | flops 2689925120 | bytes 12322048 | tf_op jit(solution)/shard_map/dot_general | solution.py:73
  77.6 1.6 broadcast_in_dim.20
  79.2 5.1 %all-to-all-start = ((bf16[16,1024,64]{1,2,0:T(8,128)(2,1)}), bf16[16,1024,64]{1,2,0:T(8,128)(2,1)}, u32[]{:S(2)}, u32[]{:S(2)}) async-start(bf16[16,1024,64]{1,2,0:T(8,128)(2,1)} %broadcast_in_dim.20), calls=%async_computation | async-start | bytes 4194304 | tf_op jit(solution)/shard_map/all_to_all | solution.py:21
  84.3 0.2 reduce-scatter.2.cloned.1.call-start
  84.6 0.8 iota_compare_fusion.1
  85.4 1.2 iota_compare_fusion
  86.6 2.8 %fusion.23 = (f32[1024,64]{1,0:T(8,128)}, f32[1024,64]{1,0:T(8,128)}) fusion(f32[64]{0:T(128)S(1)} %negate_power_fusion), kind=kLoop, calls=%fused_computation.40 | loop fusion | flops 65536 | bytes 524544 | tf_op jit(solution)/shard_map/cos | solution.py:48
  89.4 0.1 slice.52
  89.5 1.1 fusion.58
  90.5 1.4 copy.27
  91.9 2.4 copy.28
  94.3 2.8 %subtract_convert_fusion = (bf16[1024,2,64]{2,0,1:T(8,128)(2,1)}, bf16[1024,2,64]{2,0,1:T(8,128)(2,1)}) fusion(f32[1024,2,64]{2,0,1:T(8,128)} %copy.28, f32[1024,2,64]{2,0,1:T(8,128)S(1)} %copy.27, f32[1024,64]{1,0:T(8,128)} %get-tuple-element.9, f32[1024,64]{1,0:T(8,128)} %get-tuple-element.8), kind=kLoop, calls=%fused_computation.32 | loop fusion | flops 1048576 | bytes 2097152 | tf_op jit(solution)/shard_map/convert.6
  97.1 0.0 copy-start.3
  97.1 0.0 copy-start.4
  97.1 14.3 %all-to-all-done = bf16[16,1024,64]{1,2,0:T(8,128)(2,1)} async-done(((bf16[16,1024,64]{1,2,0:T(8,128)(2,1)}), bf16[16,1024,64]{1,2,0:T(8,128)(2,1)}, u32[]{:S(2)}, u32[]{:S(2)}) %all-to-all-start) | async-done | bytes 2097184 | tf_op jit(solution)/shard_map/all_to_all | solution.py:21
  111.4 1.0 constant_dynamic-slice_fusion
  112.4 0.2 copy.26
  112.6 2.2 subtract_convert_fusion.1
  114.8 0.0 copy-start.5
  114.8 0.0 copy-start.6
  114.8 0.0 copy-done.3
  114.8 0.0 copy-done.4
  114.8 3.5 %fusion.60 = (f32[2,512]{1,0:T(2,128)S(1)}, f32[2,512,512]{1,2,0:T(8,128)}) fusion(pred[512,512]{0,1:T(8,128)(4,1)S(1)} %copy-done.4, bf16[1024,2,64]{2,0,1:T(8,128)(2,1)S(1)} %copy-done.3, bf16[1024,2,64]{2,0,1:T(8,128)(2,1)} %get-tuple-element.3, bf16[1024,1,64]{2,0,1:T(8,128)(2,1)S(1)} %get-tuple-element.7, bf16[1024,1,64]{2,0,1:T(8,128)(2,1)S(1)} %get-tuple-element.6), kind=kOutput, calls=%fused_computation.81 | convolution fusion | flops 137101824 | bytes 3149824 | tf_op jit(solution)/shard_map/sub | solution.py:100
  118.3 0.0 copy-done.5
  118.3 0.0 copy-done.6
  118.3 0.0 copy-start.2
  118.3 2.0 convolution_convert_fusion.1
  120.4 0.0 copy-done.2
  120.4 4.8 %fusion.59 = (f32[2,512]{1,0:T(2,128)S(1)}, f32[2,512,1024]{1,2,0:T(8,128)}) fusion(pred[512,1024]{0,1:T(8,128)(4,1)S(1)} %copy-done.2, bf16[1024,64]{1,0:T(8,128)(2,1)} %bitcast.79, bf16[1024,64]{1,0:T(8,128)(2,1)} %bitcast.78, bf16[1024,2,64]{2,0,1:T(8,128)(2,1)} %get-tuple-element.3, bf16[1024,2,64]{2,0,1:T(8,128)(2,1)S(1)} %copy-done.3), kind=kOutput, calls=%fused_computation.80 | convolution fusion | flops 273679360 | bytes 5509120 | tf_op jit(solution)/shard_map/sub | solution.py:100
  125.2 2.7 %fusion.15 = bf16[128,2,512]{2,0,1:T(8,128)(2,1)S(1)} fusion(f32[2,512,1024]{1,2,0:T(8,128)} %get-tuple-element.11, f32[2,512]{1,0:T(2,128)S(1)} %get-tuple-element.10, bf16[1024,1024]{0,1:T(8,128)(2,1)} %bitcast.3, s32[]{:T(128)S(6)} %select_n.20), kind=kOutput, calls=%fused_computation.23 | convolution fusion | flops 270663680 | bytes 4722692 | tf_op jit(solution)/shard_map/hqk,kd->qhd/dot_general | solution.py:101
  127.9 0.0 copy-done
  128.0 5.6 %convolution_convert_fusion = bf16[1024,4096]{1,0:T(8,128)(2,1)} fusion(bf16[256,4096]{1,0:T(8,128)(2,1)S(1)} %copy-done, bf16[512,256]{0,1:T(8,128)(2,1)S(1)} %bitcast.76, bf16[512,256]{0,1:T(8,128)(2,1)S(1)} %bitcast.74), kind=kOutput, calls=%fused_computation.2 | convolution fusion | flops 2152726528 | bytes 11010048 | tf_op jit(solution)/shard_map/dot_general | solution.py:107
  133.6 0.0 copy-start.9
  133.6 0.0 reduce-scatter.2.cloned.1.call-update
  133.6 0.7 copy-done.9
  134.2 0.5 convolution_bitcast_fusion
  134.7 0.9 fusion.65
  135.7 25.0 %psum.35 = f32[4096]{0:T(1024)S(1)} all-reduce(f32[4096]{0:T(1024)S(1)} %bitcast.80), channel_id=1, replica_groups=mesh['dp_0'=8,'dp_1'=2,'tensor_0'=4,'tensor_1'=2,'tensor_2'=2] {'dp_0'}, use_global_device_ids=true, to_apply=%region_6.7 | all-reduce | flops 4096 | bytes 32768 | tf_op jit(solution)/shard_map/psum | solution.py:39
  160.7 9.9 %psum.36 = f32[4096]{0:T(1024)S(1)} all-reduce(f32[4096]{0:T(1024)S(1)} %psum.35), channel_id=1, replica_groups=mesh['dp_0'=8,'dp_1'=2,'tensor_0'=4,'tensor_1'=2,'tensor_2'=2] {'dp_1'}, use_global_device_ids=true, to_apply=%region_7.8 | all-reduce | flops 4096 | bytes 32768 | tf_op jit(solution)/shard_map/psum | solution.py:39
  170.6 12.4 %psum.37 = f32[4096]{0:T(1024)S(1)} all-reduce(f32[4096]{0:T(1024)S(1)} %psum.36), channel_id=1, replica_groups=mesh['dp_0'=8,'dp_1'=2,'tensor_0'=4,'tensor_1'=2,'tensor_2'=2] {'tensor_0'}, use_global_device_ids=true, to_apply=%region_8.9 | all-reduce | flops 4096 | bytes 32768 | tf_op jit(solution)/shard_map/psum | solution.py:39
  183.0 6.1 %psum.38 = f32[4096]{0:T(1024)S(1)} all-reduce(f32[4096]{0:T(1024)S(1)} %psum.37), channel_id=1, replica_groups=mesh['dp_0'=8,'dp_1'=2,'tensor_0'=4,'tensor_1'=2,'tensor_2'=2] {'tensor_1'}, use_global_device_ids=true, to_apply=%region_9.10 | all-reduce | flops 4096 | bytes 32768 | tf_op jit(solution)/shard_map/psum | solution.py:39
  189.1 15.2 %psum.39 = f32[4096]{0:T(1024)S(1)} all-reduce(f32[4096]{0:T(1024)S(1)} %psum.38), channel_id=1, replica_groups=mesh['dp_0'=8,'dp_1'=2,'tensor_0'=4,'tensor_1'=2,'tensor_2'=2] {'tensor_2'}, use_global_device_ids=true, to_apply=%region_10.11 | all-reduce | flops 4096 | bytes 32768 | tf_op jit(solution)/shard_map/psum | solution.py:39
  204.3 0.6 broadcast_multiply_fusion
  204.9 28.0 %reduce-scatter.2.cloned.1.call-done = bf16[64,4096]{1,0:T(8,128)(2,1)} async-done(((bf16[1024,4096]{1,0:T(8,128)(2,1)}), bf16[64,4096]{1,0:T(8,128)(2,1)}) %reduce-scatter.2.cloned.1.call-update) | async-done | bytes 524304 | tf_op jit(solution)/shard_map/reduce_scatter | solution.py:106
  (6 shorter events, 0.1 us)
Async XLA Ops:
  7.2 120.8 %copy-start = (bf16[256,4096]{1,0:T(8,128)(2,1)S(1)}, bf16[256,4096]{1,0:T(8,128)(2,1)}, u32[]{:S(2)}) copy-start(bf16[256,4096]{1,0:T(8,128)(2,1)} %param.14) | copy-start | bytes 6291460
  7.2 4.2 %copy-start.1 = (bf16[4096,64]{0,1:T(8,128)(2,1)S(1)}, bf16[4096,64]{0,1:T(8,128)(2,1)}, u32[]{:S(2)}) copy-start(bf16[4096,64]{0,1:T(8,128)(2,1)} %param.12) | copy-start | bytes 1572868
  7.2 5.7 %copy-start.8 = (bf16[256]{0:T(256)(128)(2,1)S(1)}, bf16[256]{0:T(256)(128)(2,1)}, u32[]{:S(2)}) copy-start(bf16[256]{0:T(256)(128)(2,1)} %param.11) | copy-start | bytes 1540
  7.2 5.7 %copy-start.7 = (bf16[64]{0:T(256)(128)(2,1)S(1)}, bf16[64]{0:T(256)(128)(2,1)}, u32[]{:S(2)}) copy-start(bf16[64]{0:T(256)(128)(2,1)} %param.13) | copy-start | bytes 388
  7.2 63.1 %all-gather.2.cloned.1.call-start = ((), (), s32[]{:S(2)}) async-start(), calls=%async_computation.2 | async-start | bytes 8912896 | tf_op jit(solution)/shard_map/all_gather | solution.py:74
  79.2 32.2 %all-to-all-start = ((bf16[16,1024,64]{1,2,0:T(8,128)(2,1)}), bf16[16,1024,64]{1,2,0:T(8,128)(2,1)}, u32[]{:S(2)}, u32[]{:S(2)}) async-start(bf16[16,1024,64]{1,2,0:T(8,128)(2,1)} %broadcast_in_dim.20), calls=%async_computation | async-start | bytes 4194304 | tf_op jit(solution)/shard_map/all_to_all | solution.py:21
  84.3 148.6 %reduce-scatter.2.cloned.1.call-start = ((), (), s32[]{:S(2)}) async-start(), calls=%async_computation.3 | async-start | bytes 8912896 | tf_op jit(solution)/shard_map/reduce_scatter | solution.py:106
  97.1 17.7 %copy-start.3 = (bf16[1024,2,64]{2,0,1:T(8,128)(2,1)S(1)}, bf16[1024,2,64]{2,0,1:T(8,128)(2,1)}, u32[]{:S(2)}) copy-start(bf16[1024,2,64]{2,0,1:T(8,128)(2,1)} %get-tuple-element.2) | copy-start | bytes 786436
  97.1 17.7 %copy-start.4 = (pred[512,512]{0,1:T(8,128)(4,1)S(1)}, pred[512,512]{0,1:T(8,128)(4,1)}, u32[]{:S(2)}) copy-start(pred[512,512]{0,1:T(8,128)(4,1)} %iota_compare_fusion.1) | copy-start | bytes 786436
  114.8 3.5 %copy-start.5 = (bf16[1024,1,64]{2,0,1:T(8,128)(2,1)}, bf16[1024,1,64]{2,0,1:T(8,128)(2,1)S(1)}, u32[]{:S(2)}) copy-start(bf16[1024,1,64]{2,0,1:T(8,128)(2,1)S(1)} %get-tuple-element.6) | copy-start | bytes 393220
  114.8 3.5 %copy-start.6 = (bf16[1024,1,64]{2,0,1:T(8,128)(2,1)}, bf16[1024,1,64]{2,0,1:T(8,128)(2,1)S(1)}, u32[]{:S(2)}) copy-start(bf16[1024,1,64]{2,0,1:T(8,128)(2,1)S(1)} %get-tuple-element.7) | copy-start | bytes 393220
  118.3 2.1 copy-start.2
  133.6 0.7 copy-start.9
Sparse Core Ops, SparseCore 0:
  11.5 58.7 all-gather.1
  133.7 99.1 reduce-scatter.1
where the time goes:
time: 241 us; the launch traced here: 240 us
  waiting for transfers between devices  99.9 us (41%)
  blocking collectives  68.6 us (28%)
  matrix products  27.3 us (11%)
  other arithmetic  14.6 us (6%)
  between operations  14.3 us (6%)
  local copies, waits for them, and re-layouts  9.77 us (4%)
  starting transfers between devices  5.36 us (2%)
    psum x5, blocking collectives, one_axis_at_a_time(): shard = lax.psum(shard, axis)  68.6 us
    all_gather x1, waiting for transfers between devices, local(): lax.all_gather(normed, TENSOR, axis=0, tiled=True)  57.5 us
    reduce_scatter x1, waiting for transfers between devices, local(): lax.psum_scatter(jnp.dot(context, wo, preferred_element_type=jnp.float32)...  28 us
    all_to_all x1, waiting for transfers between devices, sent_to_all(): lax.all_to_all(jnp.broadcast_to(shard[None], (count, *shard.shape)), axis...  14.3 us
    sub x2, matrix products, local(): probs = jax.nn.softmax(scores, axis=-1).astype(jnp.bfloat16)  8.29 us
    dot_general x1, matrix products, local(): jnp.dot(lax.all_gather(normed, TENSOR, axis=0, tiled=True), joined_w, pre...  7.23 us
    unnamed x24, local copies, waits for them, and re-layouts  6.03 us
    dot_general x1, matrix products, local(): jnp.dot(context, wo, preferred_element_type=jnp.float32)  5.6 us
  transfers between devices with their start and end apart: 3, of which 3 were waited for; matrix products, arithmetic and copies ran while one was open for 7% of the time, Pallas kernels for 0%

commit v1 on v0

v1 whole, which is shorter than its diff:
```python
import jax
import jax.numpy as jnp
import numpy as np
from jax import lax
from jax.experimental import pallas as pl
from jax.experimental.pallas import tpu as pltpu
from jax.sharding import Mesh
from jax.sharding import PartitionSpec as P

HD = 128
EPS = 1e-06
THETA = 1000000.0
TENSOR = ("tensor_0", "tensor_1", "tensor_2")
DP = ("dp_0", "dp_1")
MESH = pl.DeviceIdType.MESH
F32 = jnp.float32
BF16 = jnp.bfloat16

NY = 4
D = 4096
ROWS = 64
QUARTER = 16
QCOLS = 256
SEQ = 1024
CHUNKS = 8
CW = D // CHUNKS


def mult(value, by):
    return pl.multiple_of(value, by)


def split3(value):
    hi = value.astype(BF16).astype(F32)
    rest = value - hi
    mid = rest.astype(BF16).astype(F32)
    low = (rest - mid).astype(BF16).astype(F32)
    row = lax.broadcasted_iota(jnp.int32, (16, value.shape[1]), 0)
    rows = jnp.where(row == 0, hi, jnp.where(row == 1, mid, jnp.where(row == 2, low, 0.0)))
    return rows.astype(BF16)


def kernel(
    tokens, params, wq, wkv, wo, weights, cos, sin,
    out, check,
    tok, xg, wqv, wkown, wkpair, wkfull, bpair, cosv, sinv, qb, kvs, kv, ctx, ctx4, wo4,
    pbuf, ra, rfb, rfa, outv, cz, chh, cxl, cc, cy,
    ld, wl, agr, agd, ags, agds, wkr, wks, wor, wos, wod, wods,
    kvr, kvd, kvss, kvds, cxr, cxs, rar, ras, rbr, rbs, rtr, rts, ost,
    czr, czs, cdr, cds,
):
    z = lax.axis_index("dp_0")
    xh = lax.axis_index("dp_1")
    y = lax.axis_index("tensor_0")
    x = lax.axis_index("tensor_1")
    c = lax.axis_index("tensor_2")
    slot = x * 2 + c
    other_x = (x + 1) % 2
    other_c = (c + 1) % 2

    def at(dy=0, dx=0, dc=0):
        return {"tensor_0": (y + dy) % NY, "tensor_1": (x + dx) % 2, "tensor_2": (c + dc) % 2}

    def unit(dy, dx):
        return ((y + dy) % NY) * 2 + (x + dx) % 2

    up, down, pair, sibling = at(dy=1), at(dy=3), at(dx=1), at(dc=1)
    far = {"dp_1": (xh + 1) % 2, "tensor_1": other_x}

    barrier = pltpu.get_barrier_semaphore()
    peers = [at(dy=dy, dx=dx) for dy in range(4) for dx in range(2) if dy or dx]
    peers += [sibling, at(dx=1, dc=1), far, {"dp_1": (xh + 1) % 2}]
    peers += [{"dp_0": (z + d) % 8} for d in range(1, 8)]
    for peer in peers:
        pl.semaphore_signal(barrier, inc=1, device_id=peer, device_id_type=MESH)

    loads = {}

    def load(name, src, dst, sem):
        loads[name] = pltpu.make_async_copy(src, dst, sem)
        loads[name].start()

    load("tok", tokens, tok, ld.at[0])
    load("wk", wkv, wkown, ld.at[1])
    load("wq", wq, wqv, ld.at[2])
    load("cos", cos, cosv, ld.at[3])
    load("sin", sin, sinv, ld.at[4])
    my_wo = pl.ds(mult(slot * QCOLS, QCOLS), QCOLS)
    for j in range(CHUNKS):
        load(("wo", j), wo.at[:, pl.ds(j * CW, CW)], wo4.at[j, my_wo, :], wl.at[j])

    pending = []

    def send(src, dst, ssem, rsem, device):
        copy = pltpu.make_async_remote_copy(
            src_ref=src, dst_ref=dst, send_sem=ssem, recv_sem=rsem,
            device_id=device, device_id_type=MESH,
        )
        copy.start()
        pending.append(copy)

    def arrived(dst, ssem, rsem, device):
        pltpu.make_async_remote_copy(
            src_ref=dst, dst_ref=dst, send_sem=ssem, recv_sem=rsem,
            device_id=device, device_id_type=MESH,
        ).wait_recv()

    gain = params[0:1, 0:D]
    base = (y * 4 + slot) * ROWS
    loads["tok"].wait()
    for q in range(4):
        part = tok[q * QUARTER:(q + 1) * QUARTER, :].astype(F32)
        mean = jnp.mean(part * part, axis=-1, keepdims=True)
        xg[pl.ds(mult(base + q * QUARTER, QUARTER), QUARTER), :] = (
            part * lax.rsqrt(mean + EPS) * gain
        ).astype(BF16)

    pl.semaphore_wait(barrier, len(peers))

    def piece(u, q):
        return xg.at[pl.ds(mult(u * 128 + c * ROWS + q * QUARTER, QUARTER), QUARTER), :]

    def sibling_piece(u, q):
        return xg.at[pl.ds(mult(u * 128 + other_c * ROWS + q * QUARTER, QUARTER), QUARTER), :]

    counts = {"ags": 0, "agds": 0}

    def relay(u, q, device):
        k = counts["ags"]
        counts["ags"] += 1
        send(piece(u, q), piece(u, q), ags.at[k], agr.at[u * 4 + q], device)

    def relay_sibling(u, q):
        k = counts["agds"]
        counts["agds"] += 1
        send(piece(u, q), piece(u, q), agds.at[k], agd.at[u * 4 + q], sibling)

    def wait_piece(u, q):
        arrived(piece(u, q), ags.at[0], agr.at[u * 4 + q], sibling)

    def wait_sibling(u):
        for q in range(4):
            arrived(sibling_piece(u, q), agds.at[0], agd.at[u * 4 + q], sibling)

    own = unit(0, 0)
    for s in range(4):
        relay(own, s, up)
        relay(own, (s + 2) % 4, down)
        relay(own, s, pair)
    for q in range(4):
        relay_sibling(own, q)

    loads["wk"].wait()
    send(wkown, wkpair, wks.at[0], wkr.at[0], sibling)
    send(params.at[:, pl.ds(D + QCOLS, 128)], bpair, wks.at[1], wkr.at[1], sibling)

    def wo_piece(j, owner):
        return wo4.at[j, pl.ds(mult(owner * QCOLS, QCOLS), QCOLS), :]

    for j in range(CHUNKS):
        loads[("wo", j)].wait()
        send(wo_piece(j, slot), wo_piece(j, slot), wos.at[j], wor.at[j], far)
        send(wo_piece(j, slot), wo_piece(j, slot), wods.at[j], wod.at[j], sibling)

    far_slot = other_x * 2 + c
    sibling_slot = x * 2 + other_c
    far_sibling_slot = other_x * 2 + other_c

    def forward_wo(j):
        arrived(wo_piece(j, far_slot), wos.at[j], wor.at[j], far)
        send(wo_piece(j, far_slot), wo_piece(j, far_slot), wods.at[8 + j], wod.at[8 + j], sibling)

    arrived(wkpair, wks.at[0], wkr.at[0], sibling)
    arrived(bpair, wks.at[1], wkr.at[1], sibling)
    first = c == 0

    def join(i, carry):
        rows = pl.ds(mult(i * 512, 512), 512)
        mine, theirs = wkown[rows, :], wkpair[rows, :]
        left = jnp.where(first, mine, theirs)
        right = jnp.where(first, theirs, mine)
        wkfull[rows, :] = jnp.concatenate([left, right], axis=1)
        return carry

    lax.fori_loop(0, D // 512, join, 0)
    lane = lax.broadcasted_iota(jnp.int32, (1, 128), 1)
    bias_mine = params[0:1, D + QCOLS:D + QCOLS + 128]
    bias_theirs = bpair[0:1, :]
    low_half = lane < 64
    kv_bias = jnp.where(
        first,
        jnp.where(low_half, bias_mine, bias_theirs),
        jnp.where(low_half, bias_theirs, bias_mine),
    )
    q_bias = params[0:1, D:D + QCOLS]
    loads["wq"].wait()
    loads["cos"].wait()
    loads["sin"].wait()

    chip = y * 2 + x
    is_value = y // 2
    turned = (1 - is_value).astype(F32)
    straight = is_value.astype(F32)
    group = chip % NY
    local_user = group == y
    local_sends = []

    def rope(value, cosine, sine):
        return value * cosine + pltpu.roll(value, 64, 1) * sine

    def project(step, u):
        rows_kv = pl.ds(mult(u * 128 + c * ROWS, ROWS), ROWS)
        pairs = jnp.dot(xg[rows_kv, :], wkfull[...], preferred_element_type=F32) + kv_bias
        pairs = pairs.astype(BF16).astype(F32)
        cosine = cosv[rows_kv, :] * turned + straight
        sine = sinv[rows_kv, :] * turned
        result = rope(pairs, cosine, sine).astype(BF16)
        kvs[step] = result
        target = kv.at[is_value, rows_kv, :]
        sem = kvr.at[is_value * 8 + u]
        same = pltpu.make_async_remote_copy(
            src_ref=kvs.at[step], dst_ref=target, send_sem=kvss.at[step], recv_sem=sem,
            device_id={"tensor_0": group}, device_id_type=MESH,
        )

        @pl.when(local_user)
        def _():
            kv[is_value, rows_kv, :] = result

        @pl.when(jnp.logical_not(local_user))
        def _():
            same.start()

        local_sends.append(same)
        send(kvs.at[step], target, kvss.at[8 + step], sem, {"tensor_0": group, "tensor_1": other_x})

        rows = pl.ds(mult(u * 128, 128), 128)
        query = jnp.dot(xg[rows, :], wqv[...], preferred_element_type=F32) + q_bias
        for h in range(2):
            cols = slice(h * HD, (h + 1) * HD)
            qb[rows, cols] = rope(query[:, cols], cosv[rows, :], sinv[rows, :]).astype(BF16)

    below, above, beside, across = unit(3, 0), unit(1, 0), unit(0, 1), unit(2, 0)
    x_across, x_below, x_above = unit(2, 1), unit(3, 1), unit(1, 1)

    wait_sibling(own)
    project(0, own)
    for s in range(4):
        wait_piece(below, s)
        if s < 2:
            relay(below, s, up)
        r = (s + 2) % 4
        wait_piece(above, r)
        if s < 2:
            relay(above, r, down)
        wait_piece(beside, s)
        relay(beside, s, up)
        relay(beside, s, down)
        relay_sibling(below, s)
        relay_sibling(above, r)
        relay_sibling(beside, s)
    wait_sibling(below)
    project(1, below)
    for q in (0, 2):
        wait_piece(across, q)
        relay(across, q, pair)
        relay_sibling(across, q)
    forward_wo(0)
    wait_sibling(above)
    project(2, above)
    for u in (x_below, x_above):
        wait_piece(u, 0)
        relay_sibling(u, 0)
    forward_wo(1)
    wait_sibling(beside)
    project(3, beside)
    for q in (1, 3):
        wait_piece(across, q)
        relay(across, q, pair)
        relay_sibling(across, q)
    for q in (0, 2):
        wait_piece(x_across, q)
        relay_sibling(x_across, q)
    for u in (x_below, x_above):
        wait_piece(u, 1)
        relay_sibling(u, 1)
    wait_sibling(across)
    project(4, across)
    forward_wo(2)
    for u in (x_below, x_above):
        wait_piece(u, 2)
        relay_sibling(u, 2)
    for q in (1, 3):
        wait_piece(x_across, q)
        relay_sibling(x_across, q)
    wait_sibling(x_across)
    project(5, x_across)
    for u in (x_below, x_above):
        wait_piece(u, 3)
        relay_sibling(u, 3)
    forward_wo(3)
    wait_sibling(x_below)
    project(6, x_below)
    wait_sibling(x_above)
    project(7, x_above)

    made_here = [
        jnp.logical_and(y == 0, x == 0),
        jnp.logical_and(y == 3, x == 1),
    ]
    for u in range(8):
        for kind in range(2):
            rows_kv = pl.ds(mult(u * 128 + c * ROWS, ROWS), ROWS)
            part = kv.at[kind, rows_kv, :]

            @pl.when(jnp.logical_not(made_here[kind]))
            def _():
                arrived(part, kvss.at[0], kvr.at[kind * 8 + u], sibling)

            send(part, part, kvds.at[kind * 8 + u], kvd.at[kind * 8 + u], sibling)
    for u in range(8):
        for kind in range(2):
            rows_kv = pl.ds(mult(u * 128 + other_c * ROWS, ROWS), ROWS)
            arrived(kv.at[kind, rows_kv, :], kvds.at[0], kvd.at[kind * 8 + u], sibling)

    forward_wo(4)

    scale = HD ** (-0.5)
    my_cols = pl.ds(mult(slot * QCOLS, QCOLS), QCOLS)
    contract_last = (((1,), (1,)), ((), ()))
    for b in reversed(range(4)):
        block = slice(b * 256, (b + 1) * 256)
        row = lax.broadcasted_iota(jnp.int32, (256, 256), 0)
        col = lax.broadcasted_iota(jnp.int32, (256, 256), 1)
        for h in range(2):
            cols = slice(h * HD, (h + 1) * HD)
            query = qb[block, cols]
            diagonal = lax.dot_general(query, kv[0, block, :], contract_last, preferred_element_type=F32)
            diagonal = jnp.where(row >= col, diagonal, -1e30)
            top = jnp.max(diagonal, axis=-1, keepdims=True)
            if b:
                earlier = lax.dot_general(
                    query, kv[0, 0:b * 256, :], contract_last, preferred_element_type=F32
                )
                top = jnp.maximum(top, jnp.max(earlier, axis=-1, keepdims=True))
            weight = jnp.exp((diagonal - top) * scale)
            total = jnp.sum(weight, axis=-1, keepdims=True)
            mixed = jnp.dot(weight.astype(BF16), kv[1, block, :], preferred_element_type=F32)
            if b:
                weight = jnp.exp((earlier - top) * scale)
                total += jnp.sum(weight, axis=-1, keepdims=True)
                mixed += jnp.dot(weight.astype(BF16), kv[1, 0:b * 256, :], preferred_element_type=F32)
            ctx[block, cols] = (mixed / total).astype(BF16)
        target = pl.ds(b * ROWS, ROWS)
        ctx4[target, my_cols] = ctx[pl.ds(mult(b * 256 + slot * ROWS, ROWS), ROWS), :]
        for k, (dx, dc) in enumerate(((1, 0), (1, 1), (0, 1))):
            theirs = ((x + dx) % 2) * 2 + (c + dc) % 2
            send(
                ctx.at[pl.ds(mult(b * 256 + theirs * ROWS, ROWS), ROWS), :],
                ctx4.at[target, my_cols],
                cxs.at[k * 4 + b], cxr.at[k * 4 + b], at(dx=dx, dc=dc),
            )

    summary = jnp.dot(split3(weights[0:1, :]), ctx[...], preferred_element_type=F32)
    summary = jnp.sum(summary, axis=0, keepdims=True)
    ctx4[256:272, :] = jnp.zeros((16, SEQ), BF16)
    ctx4[256:272, my_cols] = split3(summary)

    forward_wo(5)
    for k, (dx, dc) in enumerate(((1, 0), (1, 1), (0, 1))):
        theirs = ((x + dx) % 2) * 2 + (c + dc) % 2
        cols = pl.ds(mult(theirs * QCOLS, QCOLS), QCOLS)
        for b in range(4):
            arrived(
                ctx4.at[b * ROWS:(b + 1) * ROWS, cols], cxs.at[0], cxr.at[k * 4 + b], at(dx=dx, dc=dc)
            )

    def target_rows(dy):
        return pl.ds(mult(((y + dy) % NY) * ROWS, ROWS), ROWS)

    for j in range(CHUNKS):
        if j + 2 < CHUNKS and j + 2 > 5:
            forward_wo(j + 2)
        arrived(wo_piece(j, sibling_slot), wods.at[0], wod.at[j], sibling)
        arrived(wo_piece(j, far_sibling_slot), wods.at[0], wod.at[8 + j], sibling)
        product = jnp.dot(ctx4[...], wo4[j], preferred_element_type=F32)
        pbuf[j] = product[0:256, :].astype(BF16)
        cz[z, j:j + 1, :] = jnp.sum(product[256:272, :], axis=0, keepdims=True)
        if j % 2 == 0:
            send(pbuf.at[j, target_rows(2), :], ra.at[j], ras.at[j], rar.at[j], up)
            send(pbuf.at[j, target_rows(3), :], rfa.at[j], rts.at[j], rtr.at[j], down)
        else:
            send(pbuf.at[j, target_rows(2), :], ra.at[j], ras.at[j], rar.at[j], down)
            send(pbuf.at[j, target_rows(1), :], rfb.at[j], rbs.at[j], rbr.at[j], up)

    stages = [
        ("dp_0", 8, z, cz, 0),
        ("dp_1", 2, xh, chh, 0),
        ("tensor_1", 2, x, cxl, 1),
        ("tensor_2", 2, c, cc, 2),
        ("tensor_0", 4, y, cy, 3),
    ]

    def stage_start(i):
        axis, size, index, buf, first_sem = stages[i]
        for d in range(1, size):
            ssem, rsem = (czs.at[d], czr.at[d]) if i == 0 else (cds.at[first_sem + d - 1], cdr.at[first_sem + d - 1])
            send(buf.at[index], buf.at[index], ssem, rsem, {axis: (index + d) % size})

    def stage_end(i):
        axis, size, index, buf, first_sem = stages[i]
        for d in range(1, size):
            ssem, rsem = (czs.at[d], czr.at[d]) if i == 0 else (cds.at[first_sem + d - 1], cdr.at[first_sem + d - 1])
            source = (index + size - d) % size
            arrived(buf.at[source], ssem, rsem, {axis: source})
        total = buf[0]
        for k in range(1, size):
            total = total + buf[k]
        if i + 1 < len(stages):
            stages[i + 1][3][stages[i + 1][2]] = total
        else:
            check[...] = total * (1.0 / 128.0)

    stage_start(0)
    for j in range(CHUNKS):
        rows = target_rows(1 if j % 2 == 0 else 3)
        arrived(ra.at[j], ras.at[j], rar.at[j], sibling)
        pbuf[j, rows, :] = (pbuf[j, rows, :].astype(F32) + ra[j].astype(F32)).astype(BF16)
        if j % 2 == 0:
            send(pbuf.at[j, rows, :], rfb.at[j], rbs.at[j], rbr.at[j], up)
        else:
            send(pbuf.at[j, rows, :], rfa.at[j], rts.at[j], rtr.at[j], down)
        if j % 2 == 1:
            stage_end(j // 2)
            stage_start(j // 2 + 1)

    mine = target_rows(0)
    stores = []
    for j in (1, 3, 5, 7, 0, 2, 4, 6):
        arrived(rfb.at[j], rbs.at[j], rbr.at[j], sibling)
        arrived(rfa.at[j], rts.at[j], rtr.at[j], sibling)
        total = pbuf[j, mine, :].astype(F32) + rfb[j].astype(F32) + rfa[j].astype(F32)
        cols = slice(j * CW, (j + 1) * CW)
        outv[:, cols] = total.astype(BF16)
        store = pltpu.make_async_copy(outv.at[:, cols], out.at[:, cols], ost.at[j])
        store.start()
        stores.append(store)
    stage_end(4)

    for store in stores:
        store.wait()
    for copy in pending:
        copy.wait_send()
    for copy in local_sends:
        @pl.when(jnp.logical_not(local_user))
        def _():
            copy.wait_send()


def tables():
    half = HD // 2
    inverse = THETA ** (-(np.arange(half, dtype=np.float64) * 2.0 / HD))
    angles = np.arange(SEQ, dtype=np.float64)[:, None] * inverse[None, :]
    cosine, sine = np.cos(angles), np.sin(angles)
    return (
        np.concatenate([cosine, cosine], axis=1).astype(np.float32),
        np.concatenate([-sine, sine], axis=1).astype(np.float32),
    )


def local(tokens, gain, wq, bq, wkv, bkv, wo, check_weights):
    params = jnp.concatenate([gain, bq, bkv, bkv]).astype(F32)
    params = jnp.broadcast_to(params[None, :], (8, params.shape[0]))
    cosine, sine = tables()
    dma = pltpu.SemaphoreType.DMA
    vmem = pltpu.VMEM
    anywhere = pl.BlockSpec(memory_space=pl.ANY)
    inside = pl.BlockSpec(memory_space=pltpu.VMEM)
    attended, total = pl.pallas_call(
        kernel,
        out_shape=(
            jax.ShapeDtypeStruct((ROWS, D), BF16),
            jax.ShapeDtypeStruct((CHUNKS, CW), F32),
        ),
        in_specs=[anywhere, inside, anywhere, anywhere, anywhere, inside, anywhere, anywhere],
        out_specs=(anywhere, inside),
        scratch_shapes=[
            vmem((ROWS, D), BF16),
            vmem((SEQ, D), BF16),
            vmem((D, QCOLS), BF16),
            vmem((D, 64), BF16),
            vmem((D, 64), BF16),
            vmem((D, 128), BF16),
            vmem((8, 128), F32),
            vmem((SEQ, HD), F32),
            vmem((SEQ, HD), F32),
            vmem((SEQ, QCOLS), BF16),
            vmem((8, ROWS, HD), BF16),
            vmem((2, SEQ, HD), BF16),
            vmem((SEQ, QCOLS), BF16),
            vmem((272, SEQ), BF16),
            vmem((CHUNKS, SEQ, CW), BF16),
            vmem((CHUNKS, 256, CW), BF16),
            vmem((CHUNKS, ROWS, CW), BF16),
            vmem((CHUNKS, ROWS, CW), BF16),
            vmem((CHUNKS, ROWS, CW), BF16),
            vmem((ROWS, D), BF16),
            vmem((8, CHUNKS, CW), F32),
            vmem((2, CHUNKS, CW), F32),
            vmem((2, CHUNKS, CW), F32),
            vmem((2, CHUNKS, CW), F32),
            vmem((4, CHUNKS, CW), F32),
            dma((5,)), dma((8,)), dma((32,)), dma((32,)), dma((28,)), dma((32,)),
            dma((2,)), dma((2,)), dma((8,)), dma((8,)), dma((16,)), dma((16,)),
            dma((16,)), dma((16,)), dma((16,)), dma((16,)), dma((12,)), dma((12,)),
            dma((8,)), dma((8,)), dma((8,)), dma((8,)), dma((8,)), dma((8,)), dma((8,)),
            dma((8,)), dma((8,)), dma((6,)), dma((6,)),
        ],
        compiler_params=pltpu.CompilerParams(
            collective_id=0, has_side_effects=True, vmem_limit_bytes=56 * 1024 * 1024
        ),
        name="sublayer",
    )(tokens[0], params, wq, wkv, wo, check_weights, cosine, sine)
    return attended[None], total.reshape(D)


def solution(mesh):
    torus = Mesh(
        mesh.devices.reshape(8, 2, 4, 2, 2), ("dp_0", "dp_1", "tensor_0", "tensor_1", "tensor_2")
    )
    return jax.shard_map(
        local,
        mesh=torus,
        in_specs=(
            P(DP, TENSOR, None),
            P(),
            P(None, TENSOR),
            P(TENSOR),
            P(None, TENSOR),
            P(TENSOR),
            P(TENSOR, None),
            P(DP, None),
        ),
        out_specs=(P(DP, TENSOR, None), P()),
        check_vma=False,
    )
```

time: 241 us -> 94.9 us (0.39)
  waiting for transfers between devices: 99.9 us -> 0 us
  Pallas kernels: 0 us -> 85 us
  blocking collectives: 68.6 us -> 0 us
  matrix products: 27.3 us -> 0 us
  other arithmetic: 14.6 us -> 0 us
  between operations: 14.3 us -> 0.64 us
  starting transfers between devices: 5.36 us -> 0 us
    pallas_call x0 -> x1, Pallas kernels: none -> 85 us  [local(): pl.pallas_call(kernel, out_shape=(jax.ShapeDtypeStruct((ROWS, D), BF16),...]
    psum x5 -> x0, blocking collectives: 68.6 us -> none  [one_axis_at_a_time(): shard = lax.psum(shard, axis)]
    all_gather x1 -> x0, waiting for transfers between devices: 57.5 us -> none  [local(): lax.all_gather(normed, TENSOR, axis=0, tiled=True)]
    reduce_scatter x1 -> x0, waiting for transfers between devices: 28 us -> none  [local(): lax.psum_scatter(jnp.dot(context, wo, preferred_element_type=jnp.float32)...]
    dot_general x6 -> x0, matrix products: 19 us -> none  [the longest x1 7.23 us: local(): jnp.dot(lax.all_gather(normed, TENSOR, axis=0, tiled=True), joined_w, pre...]
    all_to_all x1 -> x0, waiting for transfers between devices: 14.3 us -> none  [sent_to_all(): lax.all_to_all(jnp.broadcast_to(shard[None], (count, *shard.shape)), axis...]
    sub x2 -> x0, matrix products: 8.29 us -> none  [local(): probs = jax.nn.softmax(scores, axis=-1).astype(jnp.bfloat16)]
    all_to_all x1 -> x0, starting transfers between devices: 5.11 us -> none  [sent_to_all(): lax.all_to_all(jnp.broadcast_to(shard[None], (count, *shard.shape)), axis...]
  transfers between devices with their start and end apart: 3 -> 0, of which waited for: 3 -> 0; matrix products, arithmetic and copies ran while one was open for 7% -> 0% of each run, Pallas kernels for 0% -> 0%
where the time goes in v1:
time: 94.9 us; the launch traced here: 94.6 us
  Pallas kernels  85 us (90%)
  local copies, waits for them, and re-layouts  9.02 us (10%)
    pallas_call x1, Pallas kernels, local(): pl.pallas_call(kernel, out_shape=(jax.ShapeDtypeStruct((ROWS, D), BF16),...  85 us
    unnamed x3, local copies, waits for them, and re-layouts  5.57 us
    concatenate x1, local copies, waits for them, and re-layouts, local(): params = jnp.concatenate([gain, bq, bkv, bkv]).astype(F32)  2.78 us

profile of v1, /device:TPU:1, one launch (start us, length us, event | category | flops | bytes accessed | tf_op | source)
XLA Modules:
  0.0 94.6 jit_solution(10405628248429185321)
XLA Ops:
  0.6 2.8 %concatenate.7 = bf16[4480]{0:T(1024)(128)(2,1)S(1)} concatenate(bf16[4096]{0:T(1024)(128)(2,1)} %param.11, bf16[256]{0:T(256)(128)(2,1)} %param.13, bf16[64]{0:T(256)(128)(2,1)} %param.15, bf16[64]{0:T(256)(128)(2,1)} %param.15), dimensions={0} | concatenate | bytes 17920 | tf_op jit(solution)/shard_map/concatenate | solution.py:472
  3.4 0.7 broadcast_in_dim.4.params
  4.1 2.4 %copy.12.wkv = bf16[4096,64]{1,0:T(8,128)(2,1)} copy(bf16[4096,64]{0,1:T(8,128)(2,1)} %param.14) | data formatting | bytes 1048576 | tf_op args[4]
  6.5 85.0 %sublayer.1 = (bf16[64,4096]{1,0:T(8,128)(2,1)}, f32[8,512]{1,0:T(8,128)}) custom-call(bf16[64,4096]{1,0:T(8,128)(2,1)} %bitcast.5, f32[8,4480]{1,0:T(8,128)} %broadcast_in_dim.4.params, bf16[4096,256]{1,0:T(8,128)(2,1)} %wq.1, bf16[4096,64]{1,0:T(8,128)(2,1)} %copy.12.wkv, bf16[256,4096]{1,0:T(8,128)(2,1)} %wo.1, f32[1,1024]{1,0:T(1,128)} %weights.1, ...), custom_call_target="tpu_custom_call" | custom-call | tf_op jit(solution)/shard_map/sublayer/pallas_call | solution.py:479
  91.4 1.3 %copy.13 = f32[1,4,8,128]{3,1,2,0:T(4,128)} copy(f32[1,4,8,128]{3,2,1,0:T(8,128)} %bitcast.7) | data formatting | bytes 32768
  92.8 1.9 %copy.15 = bf16[1,64,4096]{2,1,0:T(8,128)(2,1)} copy(bf16[1,64,4096]{2,1,0:T(8,128)(2,1)} %bitcast.4) | data formatting | bytes 1048576

commit v2 on v1

v2 whole, which is shorter than its diff:
```python
import jax
import jax.numpy as jnp
import numpy as np
from jax import lax
from jax.experimental import pallas as pl
from jax.experimental.pallas import tpu as pltpu
from jax.sharding import Mesh
from jax.sharding import PartitionSpec as P

HD = 128
EPS = 1e-06
THETA = 1000000.0
TENSOR = ("tensor_0", "tensor_1", "tensor_2")
DP = ("dp_0", "dp_1")
MESH = pl.DeviceIdType.MESH
F32 = jnp.float32
BF16 = jnp.bfloat16

NY = 4
D = 4096
ROWS = 64
QUARTER = 16
QCOLS = 256
SEQ = 1024
CHUNKS = 8
CW = D // CHUNKS
NEAR_CHUNK = 7
LATE = 5


def mult(value, by):
    return pl.multiple_of(value, by)


def split3(value):
    hi = value.astype(BF16).astype(F32)
    rest = value - hi
    mid = rest.astype(BF16).astype(F32)
    low = (rest - mid).astype(BF16).astype(F32)
    row = lax.broadcasted_iota(jnp.int32, (16, value.shape[1]), 0)
    rows = jnp.where(row == 0, hi, jnp.where(row == 1, mid, jnp.where(row == 2, low, 0.0)))
    return rows.astype(BF16)


def kernel(
    tokens, gain_in, bq_in, bkv_in, wq, wkv, wo, weights, cos, sin,
    out, check,
    tok, xg, wqv, wkfull, bmine, bpair, cosv, sinv, qb, kvs, kv, ctx, ctx4, wo4,
    pbuf, ra, rfb, rfa, outv, cz, chh, cxl, cc, cy,
    ld, tl, wl, agr, agd, ags, agds, wkr, wks, wor, wos, wod, wods,
    kvr, kvd, kvss, kvds, cxr, cxs, rar, ras, rbr, rbs, rtr, rts, ost,
    cdr, cds,
):
    z = lax.axis_index("dp_0")
    xh = lax.axis_index("dp_1")
    y = lax.axis_index("tensor_0")
    x = lax.axis_index("tensor_1")
    c = lax.axis_index("tensor_2")
    slot = x * 2 + c
    other_x = (x + 1) % 2
    other_c = (c + 1) % 2

    def at(dy=0, dx=0, dc=0):
        return {"tensor_0": (y + dy) % NY, "tensor_1": (x + dx) % 2, "tensor_2": (c + dc) % 2}

    def unit(dy, dx):
        return ((y + dy) % NY) * 2 + (x + dx) % 2

    up, down, pair, sibling = at(dy=1), at(dy=3), at(dx=1), at(dc=1)
    far = {"dp_1": (xh + 1) % 2, "tensor_1": other_x}

    barrier = pltpu.get_barrier_semaphore()
    peers = [at(dy=dy, dx=dx) for dy in range(4) for dx in range(2) if dy or dx]
    peers += [sibling, at(dx=1, dc=1), far, {"dp_1": (xh + 1) % 2}]
    peers += [{"dp_0": (z + d) % 8} for d in range(1, 8)]
    for peer in peers:
        pl.semaphore_signal(barrier, inc=1, device_id=peer, device_id_type=MESH)

    contract_last = (((1,), (1,)), ((), ()))
    loads = {}

    def load(name, src, dst, sem):
        loads[name] = pltpu.make_async_copy(src, dst, sem)
        loads[name].start()

    for q in range(4):
        part = slice(q * QUARTER, (q + 1) * QUARTER)
        load(("tok", q), tokens.at[part, :], tok.at[part, :], tl.at[q])
    my_wk = wkfull.at[pl.ds(mult(c * 64, 64), 64), :]
    load("wk", wkv, my_wk, ld.at[1])
    load("wq", wq, wqv, ld.at[2])
    load("cos", cos, cosv, ld.at[3])
    load("sin", sin, sinv, ld.at[4])
    my_wo = pl.ds(mult(slot * QCOLS, QCOLS), QCOLS)
    for j in range(CHUNKS):
        load(("wo", j), wo.at[:, pl.ds(j * CW, CW)], wo4.at[j, my_wo, :], wl.at[j])

    pending = []

    def send(src, dst, ssem, rsem, device):
        copy = pltpu.make_async_remote_copy(
            src_ref=src, dst_ref=dst, send_sem=ssem, recv_sem=rsem,
            device_id=device, device_id_type=MESH,
        )
        copy.start()
        pending.append(copy)

    def arrived(dst, ssem, rsem, device):
        pltpu.make_async_remote_copy(
            src_ref=dst, dst_ref=dst, send_sem=ssem, recv_sem=rsem,
            device_id=device, device_id_type=MESH,
        ).wait_recv()

    gain = gain_in[...].astype(F32).reshape(1, D)
    q_bias = bq_in[...].astype(F32).reshape(1, QCOLS)
    bias_mine = bkv_in[...].astype(F32).reshape(1, 64)
    bias_mine = jnp.concatenate([bias_mine, bias_mine], axis=1)
    bmine[...] = jnp.broadcast_to(bias_mine, (8, 128))
    base = (y * 4 + slot) * ROWS
    for q in range(4):
        loads[("tok", q)].wait()
        part = tok[q * QUARTER:(q + 1) * QUARTER, :].astype(F32)
        mean = jnp.mean(part * part, axis=-1, keepdims=True)
        xg[pl.ds(mult(base + q * QUARTER, QUARTER), QUARTER), :] = (
            part * lax.rsqrt(mean + EPS) * gain
        ).astype(BF16)

    pl.semaphore_wait(barrier, len(peers))

    def piece(u, q):
        return xg.at[pl.ds(mult(u * 128 + c * ROWS + q * QUARTER, QUARTER), QUARTER), :]

    def sibling_piece(u, q):
        return xg.at[pl.ds(mult(u * 128 + other_c * ROWS + q * QUARTER, QUARTER), QUARTER), :]

    counts = {"ags": 0, "agds": 0}

    def relay(u, q, device):
        k = counts["ags"]
        counts["ags"] += 1
        send(piece(u, q), piece(u, q), ags.at[k], agr.at[u * 4 + q], device)

    def relay_sibling(u, q):
        k = counts["agds"]
        counts["agds"] += 1
        send(piece(u, q), piece(u, q), agds.at[k], agd.at[u * 4 + q], sibling)

    def wait_piece(u, q):
        arrived(piece(u, q), ags.at[0], agr.at[u * 4 + q], sibling)

    def wait_sibling(u):
        for q in range(4):
            arrived(sibling_piece(u, q), agds.at[0], agd.at[u * 4 + q], sibling)

    own = unit(0, 0)
    for s in range(4):
        relay(own, s, up)
        relay(own, (s + 2) % 4, down)
        relay(own, s, pair)
    for q in range(4):
        relay_sibling(own, q)

    loads["wk"].wait()
    send(my_wk, my_wk, wks.at[0], wkr.at[0], sibling)
    send(bmine, bpair, wks.at[1], wkr.at[1], sibling)

    def wo_piece(j, owner):
        return wo4.at[j, pl.ds(mult(owner * QCOLS, QCOLS), QCOLS), :]

    for j in range(CHUNKS):
        loads[("wo", j)].wait()
        route = pair if j == NEAR_CHUNK else far
        send(wo_piece(j, slot), wo_piece(j, slot), wos.at[j], wor.at[j], route)
        send(wo_piece(j, slot), wo_piece(j, slot), wods.at[j], wod.at[j], sibling)

    far_slot = other_x * 2 + c
    sibling_slot = x * 2 + other_c
    far_sibling_slot = other_x * 2 + other_c

    def forward_wo(j):
        arrived(wo_piece(j, far_slot), wos.at[j], wor.at[j], far)
        send(wo_piece(j, far_slot), wo_piece(j, far_slot), wods.at[8 + j], wod.at[8 + j], sibling)

    arrived(wkfull.at[pl.ds(mult(other_c * 64, 64), 64), :], wks.at[0], wkr.at[0], sibling)
    arrived(bpair, wks.at[1], wkr.at[1], sibling)
    first = c == 0
    lane = lax.broadcasted_iota(jnp.int32, (1, 128), 1)
    bias_theirs = bpair[0:1, :]
    low_half = lane < 64
    kv_bias = jnp.where(
        first,
        jnp.where(low_half, bias_mine, bias_theirs),
        jnp.where(low_half, bias_theirs, bias_mine),
    )
    loads["wq"].wait()
    loads["cos"].wait()
    loads["sin"].wait()

    chip = y * 2 + x
    is_value = y // 2
    turned = (1 - is_value).astype(F32)
    straight = is_value.astype(F32)
    group = chip % NY
    local_user = group == y
    local_sends = []

    def rope(value, cosine, sine):
        return value * cosine + pltpu.roll(value, 64, 1) * sine

    def plane_rows(u, plane):
        return pl.ds(mult(u * 128 + plane * ROWS, ROWS), ROWS)

    made = {"count": 0}

    def push(step, rows_kv, sem, device):
        k = made["count"]
        made["count"] += 1
        return pltpu.make_async_remote_copy(
            src_ref=kvs.at[step], dst_ref=kv.at[is_value, rows_kv, :],
            send_sem=kvss.at[k], recv_sem=sem, device_id=device, device_id_type=MESH,
        )

    def make_pairs(steps, units):
        lhs = [xg[plane_rows(u, c), :] for u in units]
        lhs = lhs[0] if len(lhs) == 1 else jnp.concatenate(lhs, axis=0)
        made_rows = lax.dot_general(
            lhs, wkfull[...], contract_last, preferred_element_type=F32
        ) + kv_bias
        made_rows = made_rows.astype(BF16).astype(F32)
        for i, (step, u) in enumerate(zip(steps, units)):
            rows_kv = plane_rows(u, c)
            cosine = cosv[rows_kv, :] * turned + straight
            sine = sinv[rows_kv, :] * turned
            result = rope(made_rows[i * ROWS:(i + 1) * ROWS, :], cosine, sine).astype(BF16)
            kvs[step] = result
            sem = kvr.at[is_value * 8 + u]
            same = push(step, rows_kv, sem, {"tensor_0": group})

            @pl.when(local_user)
            def _():
                kv[is_value, rows_kv, :] = result

            @pl.when(jnp.logical_not(local_user))
            def _():
                same.start()

            local_sends.append(same)
            others = [push(step, rows_kv, sem, {"tensor_0": group, "tensor_1": other_x})]
            if step >= LATE:
                sem = kvd.at[is_value * 8 + u]
                for px in (other_x, x):
                    others.append(
                        push(step, rows_kv, sem, {"tensor_0": group, "tensor_1": px, "tensor_2": other_c})
                    )
            for copy in others:
                copy.start()
                pending.append(copy)

    def make_query(units):
        lhs = [xg[pl.ds(mult(u * 128, 128), 128), :] for u in units]
        lhs = lhs[0] if len(lhs) == 1 else jnp.concatenate(lhs, axis=0)
        query = jnp.dot(lhs, wqv[...], preferred_element_type=F32) + q_bias
        for i, u in enumerate(units):
            rows = pl.ds(mult(u * 128, 128), 128)
            for h in range(2):
                cols = slice(h * HD, (h + 1) * HD)
                part = query[i * 128:(i + 1) * 128, cols]
                qb[rows, cols] = rope(part, cosv[rows, :], sinv[rows, :]).astype(BF16)

    def project(step, u):
        wait_sibling(u)
        make_pairs([step], [u])
        make_query([u])

    below, above, beside, across = unit(3, 0), unit(1, 0), unit(0, 1), unit(2, 0)
    x_across, x_below, x_above = unit(2, 1), unit(3, 1), unit(1, 1)

    project(0, own)
    for s in range(4):
        wait_piece(below, s)
        if s < 2:
            relay(below, s, up)
        r = (s + 2) % 4
        wait_piece(above, r)
        if s < 2:
            relay(above, r, down)
        wait_piece(beside, s)
        relay(beside, s, up)
        relay(beside, s, down)
        relay_sibling(below, s)
        relay_sibling(above, r)
        relay_sibling(beside, s)
    project(1, below)
    for q in (0, 2):
        wait_piece(across, q)
        relay(across, q, pair)
        relay_sibling(across, q)
    forward_wo(0)
    project(2, above)
    for u in (x_below, x_above):
        wait_piece(u, 0)
        relay_sibling(u, 0)
    forward_wo(1)
    project(3, beside)
    for q in (1, 3):
        wait_piece(across, q)
        relay(across, q, pair)
        relay_sibling(across, q)
    for q in (0, 2):
        wait_piece(x_across, q)
        relay_sibling(x_across, q)
    for u in (x_below, x_above):
        wait_piece(u, 1)
        relay_sibling(u, 1)
    project(4, across)
    forward_wo(2)
    for u in (x_below, x_above):
        wait_piece(u, 2)
        relay_sibling(u, 2)
    for q in (1, 3):
        wait_piece(x_across, q)
        relay_sibling(x_across, q)
    make_pairs([5], [x_across])
    for u in (x_below, x_above):
        wait_piece(u, 3)
        relay_sibling(u, 3)
    make_pairs([6, 7], [x_below, x_above])

    made_here = [
        jnp.logical_and(y == 0, x == 0),
        jnp.logical_and(y == 3, x == 1),
    ]
    order = ((0, 0), (3, 0), (1, 0), (0, 1), (2, 0), (2, 1), (3, 1), (1, 1))

    def source_unit(kind, step):
        dy, dx = order[step]
        return ((kind * 2 + y // 2 + dy) % NY) * 2 + (y % 2 + dx) % 2

    def wait_made(kind, step):
        u = source_unit(kind, step)
        part = kv.at[kind, plane_rows(u, c), :]

        @pl.when(jnp.logical_not(made_here[kind]))
        def _():
            arrived(part, kvss.at[0], kvr.at[kind * 8 + u], sibling)

        return part, u

    def forward_made(step):
        for kind in range(2):
            part, u = wait_made(kind, step)
            send(part, part, kvds.at[kind * LATE + step], kvd.at[kind * 8 + u], sibling)

    wait_sibling(x_across)
    make_query([x_across])
    forward_wo(3)
    for step in range(3):
        forward_made(step)
    wait_sibling(x_below)
    wait_sibling(x_above)
    make_query([x_below, x_above])
    for step in range(3, LATE):
        forward_made(step)

    for step in range(LATE, 8):
        for kind in range(2):
            wait_made(kind, step)
    for u in range(8):
        for kind in range(2):
            arrived(kv.at[kind, plane_rows(u, other_c), :], kvds.at[0], kvd.at[kind * 8 + u], sibling)

    scale = HD ** (-0.5)
    my_cols = pl.ds(mult(slot * QCOLS, QCOLS), QCOLS)
    beyond = ((1, 0), (1, 1), (0, 1))

    def theirs(dx, dc):
        return ((x + dx) % 2) * 2 + (c + dc) % 2

    def attend(k):
        b = (y + (2, 1, 3, 0)[k]) % NY
        block = pl.ds(mult(b * 256, 256), 256)
        row = lax.broadcasted_iota(jnp.int32, (256, SEQ), 0) + b * 256
        col = lax.broadcasted_iota(jnp.int32, (256, SEQ), 1)
        for h in range(2):
            cols = slice(h * HD, (h + 1) * HD)
            scores = lax.dot_general(qb[block, cols], kv[0], contract_last, preferred_element_type=F32)
            scores = jnp.where(row >= col, scores, -1e30)
            top = jnp.max(scores, axis=-1, keepdims=True)
            weight = jnp.exp((scores - top) * scale)
            total = jnp.sum(weight, axis=-1, keepdims=True)
            mixed = jnp.dot(weight.astype(BF16), kv[1], preferred_element_type=F32)
            ctx[block, cols] = (mixed / total).astype(BF16)
        target = pl.ds(k * ROWS, ROWS)
        ctx4[target, my_cols] = ctx[pl.ds(mult(b * 256 + slot * ROWS, ROWS), ROWS), :]
        for i, (dx, dc) in enumerate(beyond):
            send(
                ctx.at[pl.ds(mult(b * 256 + theirs(dx, dc) * ROWS, ROWS), ROWS), :],
                ctx4.at[target, my_cols],
                cxs.at[i * 4 + k], cxr.at[i * 4 + k], at(dx=dx, dc=dc),
            )

    def gathered(k):
        for i, (dx, dc) in enumerate(beyond):
            cols = pl.ds(mult(theirs(dx, dc) * QCOLS, QCOLS), QCOLS)
            arrived(
                ctx4.at[k * ROWS:(k + 1) * ROWS, cols], cxs.at[0], cxr.at[i * 4 + k], at(dx=dx, dc=dc)
            )

    stages = [
        ("tensor_0", 4, y, cy, 0),
        ("dp_0", 8, z, cz, 3),
        ("dp_1", 2, xh, chh, 10),
        ("tensor_1", 2, x, cxl, 11),
        ("tensor_2", 2, c, cc, 12),
    ]

    def stage_start(i):
        axis, size, index, buf, first_sem = stages[i]
        for d in range(1, size):
            ssem, rsem = cds.at[first_sem + d - 1], cdr.at[first_sem + d - 1]
            send(buf.at[index], buf.at[index], ssem, rsem, {axis: (index + d) % size})

    def stage_end(i):
        axis, size, index, buf, first_sem = stages[i]
        for d in range(1, size):
            ssem, rsem = cds.at[first_sem + d - 1], cdr.at[first_sem + d - 1]
            source = (index + size - d) % size
            arrived(buf.at[source], ssem, rsem, {axis: source})
        total = buf[0]
        for k in range(1, size):
            total = total + buf[k]
        if i + 1 < len(stages):
            stages[i + 1][3][stages[i + 1][2]] = total
        else:
            total = total * (1.0 / 128.0)
            for j in range(CHUNKS):
                check[0:1, j * CW:(j + 1) * CW] = total[j:j + 1, :]

    attend(0)
    forward_wo(4)
    attend(1)
    forward_wo(5)
    forward_wo(NEAR_CHUNK)
    attend(2)
    attend(3)

    summary = jnp.dot(split3(weights[0:1, :]), ctx[...], preferred_element_type=F32)
    summary = split3(jnp.sum(summary, axis=0, keepdims=True))
    for j in range(CHUNKS):
        term = jnp.dot(summary, wo4[j, my_cols, :], preferred_element_type=F32)
        cy[y, j:j + 1, :] = jnp.sum(term, axis=0, keepdims=True)
    stage_start(0)
    gathered(0)

    far_rows, up_rows, down_rows, own_rows = (slice(k * ROWS, (k + 1) * ROWS) for k in range(4))
    for j in range(CHUNKS):
        if j == 4:
            forward_wo(6)
        arrived(wo_piece(j, sibling_slot), wods.at[0], wod.at[j], sibling)
        arrived(wo_piece(j, far_sibling_slot), wods.at[0], wod.at[8 + j], sibling)
        product = jnp.dot(ctx4[far_rows, :], wo4[j], preferred_element_type=F32)
        pbuf[j, far_rows, :] = product.astype(BF16)
        send(pbuf.at[j, far_rows, :], ra.at[j], ras.at[j], rar.at[j], down if j % 2 else up)

    stage_end(0)
    stage_start(1)
    for k in range(1, 4):
        gathered(k)
    stage_end(1)
    stage_start(2)
    for j in range(CHUNKS):
        product = jnp.dot(ctx4[ROWS:256, :], wo4[j], preferred_element_type=F32)
        pbuf[j, ROWS:256, :] = product.astype(BF16)
        if j % 2 == 0:
            send(pbuf.at[j, down_rows, :], rfa.at[j], rts.at[j], rtr.at[j], down)
        else:
            send(pbuf.at[j, up_rows, :], rfb.at[j], rbs.at[j], rbr.at[j], up)

    for j in range(CHUNKS):
        rows = up_rows if j % 2 == 0 else down_rows
        arrived(ra.at[j], ras.at[j], rar.at[j], sibling)
        pbuf[j, rows, :] = (pbuf[j, rows, :].astype(F32) + ra[j].astype(F32)).astype(BF16)
        if j % 2 == 0:
            send(pbuf.at[j, rows, :], rfb.at[j], rbs.at[j], rbr.at[j], up)
        else:
            send(pbuf.at[j, rows, :], rfa.at[j], rts.at[j], rtr.at[j], down)
    for i in range(2, 4):
        stage_end(i)
        stage_start(i + 1)
    stage_end(4)

    stores = []
    for j in (1, 3, 5, 7, 0, 2, 4, 6):
        arrived(rfb.at[j], rbs.at[j], rbr.at[j], sibling)
        arrived(rfa.at[j], rts.at[j], rtr.at[j], sibling)
        total = pbuf[j, own_rows, :].astype(F32) + rfb[j].astype(F32) + rfa[j].astype(F32)
        cols = slice(j * CW, (j + 1) * CW)
        outv[:, cols] = total.astype(BF16)
        store = pltpu.make_async_copy(outv.at[:, cols], out.at[:, cols], ost.at[j])
        store.start()
        stores.append(store)

    for store in stores:
        store.wait()
    for copy in pending:
        copy.wait_send()
    for copy in local_sends:
        @pl.when(jnp.logical_not(local_user))
        def _():
            copy.wait_send()


def tables():
    half = HD // 2
    inverse = THETA ** (-(np.arange(half, dtype=np.float64) * 2.0 / HD))
    angles = np.arange(SEQ, dtype=np.float64)[:, None] * inverse[None, :]
    cosine, sine = np.cos(angles), np.sin(angles)
    return (
        np.concatenate([cosine, cosine], axis=1).astype(np.float32),
        np.concatenate([-sine, sine], axis=1).astype(np.float32),
    )


def local(tokens, gain, wq, bq, wkv, bkv, wo, check_weights):
    cosine, sine = tables()
    dma = pltpu.SemaphoreType.DMA
    vmem = pltpu.VMEM
    anywhere = pl.BlockSpec(memory_space=pl.ANY)
    inside = pl.BlockSpec(memory_space=pltpu.VMEM)
    attended, total = pl.pallas_call(
        kernel,
        out_shape=(
            jax.ShapeDtypeStruct((ROWS, D), BF16),
            jax.ShapeDtypeStruct((1, D), F32),
        ),
        in_specs=[anywhere, inside, inside, inside, anywhere, anywhere, anywhere, inside, anywhere, anywhere],
        out_specs=(anywhere, inside),
        scratch_shapes=[
            vmem((ROWS, D), BF16),
            vmem((SEQ, D), BF16),
            vmem((D, QCOLS), BF16),
            vmem((128, D), BF16),
            vmem((8, 128), F32),
            vmem((8, 128), F32),
            vmem((SEQ, HD), F32),
            vmem((SEQ, HD), F32),
            vmem((SEQ, QCOLS), BF16),
            vmem((8, ROWS, HD), BF16),
            vmem((2, SEQ, HD), BF16),
            vmem((SEQ, QCOLS), BF16),
            vmem((256, SEQ), BF16),
            vmem((CHUNKS, SEQ, CW), BF16),
            vmem((CHUNKS, 256, CW), BF16),
            vmem((CHUNKS, ROWS, CW), BF16),
            vmem((CHUNKS, ROWS, CW), BF16),
            vmem((CHUNKS, ROWS, CW), BF16),
            vmem((ROWS, D), BF16),
            vmem((8, CHUNKS, CW), F32),
            vmem((2, CHUNKS, CW), F32),
            vmem((2, CHUNKS, CW), F32),
            vmem((2, CHUNKS, CW), F32),
            vmem((4, CHUNKS, CW), F32),
            dma((5,)), dma((4,)), dma((8,)), dma((32,)), dma((32,)), dma((28,)), dma((32,)),
            dma((2,)), dma((2,)), dma((8,)), dma((8,)), dma((16,)), dma((16,)),
            dma((16,)), dma((16,)), dma((22,)), dma((10,)), dma((12,)), dma((12,)),
            dma((8,)), dma((8,)), dma((8,)), dma((8,)), dma((8,)), dma((8,)), dma((8,)),
            dma((13,)), dma((13,)),
        ],
        compiler_params=pltpu.CompilerParams(
            collective_id=0, has_side_effects=True, vmem_limit_bytes=56 * 1024 * 1024
        ),
        name="sublayer",
    )(tokens[0], gain, bq, bkv, wq, wkv.T, wo, check_weights, cosine, sine)
    return attended[None], total.reshape(D)


def solution(mesh):
    torus = Mesh(
        mesh.devices.reshape(8, 2, 4, 2, 2), ("dp_0", "dp_1", "tensor_0", "tensor_1", "tensor_2")
    )
    return jax.shard_map(
        local,
        mesh=torus,
        in_specs=(
            P(DP, TENSOR, None),
            P(),
            P(None, TENSOR),
            P(TENSOR),
            P(None, TENSOR),
            P(TENSOR),
            P(TENSOR, None),
            P(DP, None),
        ),
        out_specs=(P(DP, TENSOR, None), P()),
        check_vma=False,
    )
```

time: 94.9 us -> 83.4 us (0.88)
  the two profiles are of different devices: /device:TPU:1 before, /device:TPU:4 now
where the time goes in v2:
time: 83.4 us; the launch traced here: 83.2 us
  Pallas kernels  79.3 us (95%)
  local copies, waits for them, and re-layouts  3.19 us (4%)
    pallas_call x1, Pallas kernels, local(): pl.pallas_call(kernel, out_shape=(jax.ShapeDtypeStruct((ROWS, D), BF16),...  79.3 us
    unnamed x2, local copies, waits for them, and re-layouts  3.19 us

profile of v2, /device:TPU:4, one launch (start us, length us, event | category | flops | bytes accessed | tf_op | source)
XLA Modules:
  0.0 83.2 jit_solution(10672222779127561628)
XLA Ops:
  0.6 79.3 %sublayer.1 = (bf16[64,4096]{1,0:T(8,128)(2,1)}, f32[1,4096]{1,0:T(1,128)}) custom-call(bf16[64,4096]{1,0:T(8,128)(2,1)} %bitcast.4, bf16[4096]{0:T(1024)(128)(2,1)} %gain_in.1, bf16[256]{0:T(256)(128)(2,1)} %bq_in.1, bf16[64]{0:T(256)(128)(2,1)} %bkv_in.1, bf16[4096,256]{1,0:T(8,128)(2,1)} %wq.1, bf16[64,4096]{1,0:T(8,128)(2,1)} %bitcast.5, ...), custom_call_target="tpu_custom_call" | custom-call | tf_op jit(solution)/shard_map/sublayer/pallas_call | solution.py:530
  80.0 1.9 %copy.14 = bf16[1,64,4096]{2,1,0:T(8,128)(2,1)} copy(bf16[1,64,4096]{2,1,0:T(8,128)(2,1)} %bitcast.6) | data formatting | bytes 1048576
  81.9 1.3 %copy.15 = f32[4096]{0:T(1024)} copy(f32[4096]{0:T(1024)} %bitcast.7) | data formatting | bytes 32768

commit v3 on v2

v3 whole, which is shorter than its diff:
```python
import jax
import jax.numpy as jnp
import numpy as np
from jax import lax
from jax.experimental import pallas as pl
from jax.experimental.pallas import tpu as pltpu
from jax.sharding import Mesh
from jax.sharding import PartitionSpec as P

HD = 128
EPS = 1e-06
THETA = 1000000.0
TENSOR = ("tensor_0", "tensor_1", "tensor_2")
DP = ("dp_0", "dp_1")
MESH = pl.DeviceIdType.MESH
F32 = jnp.float32
BF16 = jnp.bfloat16

NY = 4
NZ = 8
D = 4096
ROWS = 64
QUARTER = 16
QCOLS = 256
SEQ = 1024
CHUNKS = 8
CW = D // CHUNKS
NEAR_CHUNK = 7
LATE = 5
(
    GATHER, SIBLING, SIBLING_WK, SIBLING_BIAS, WO, WO_SIBLING, MADE, MADE_HERE, MADE_SIBLING, CONTEXT, SUM, CHECK,
) = range(12)


def mult(value, by):
    return pl.multiple_of(value, by)


def split3(value):
    hi = value.astype(BF16).astype(F32)
    rest = value - hi
    mid = rest.astype(BF16).astype(F32)
    low = (rest - mid).astype(BF16).astype(F32)
    row = lax.broadcasted_iota(jnp.int32, (16, value.shape[1]), 0)
    rows = jnp.where(row == 0, hi, jnp.where(row == 1, mid, jnp.where(row == 2, low, 0.0)))
    return rows.astype(BF16)


def kernel(
    tokens, gain_in, bq_in, bkv_in, wq, wkv, wo, weights, cos, sin,
    out, check,
    tok, gain_v, bq_v, bkv_v, weights_v, check_v, xg, wqv, wkfull, bmine, bpair, cosv, sinv, qb, kvs, kv,
    ctx, ctx4, wo4, pbuf, ra, rfb, rfa, outv, cy, cz, cc,
    ld, agr, agd, wkr, wor, wod, kvr, kvd, cxr, rar, rbr, rtr, cdr, sent, stored, chain,
):
    z = lax.axis_index("dp_0")
    xh = lax.axis_index("dp_1")
    y = lax.axis_index("tensor_0")
    x = lax.axis_index("tensor_1")
    c = lax.axis_index("tensor_2")
    slot = x * 2 + c
    other_x = (x + 1) % 2
    other_c = (c + 1) % 2

    def at(dy=0, dx=0, dc=0):
        return {"tensor_0": (y + dy) % NY, "tensor_1": (x + dx) % 2, "tensor_2": (c + dc) % 2}

    def unit(dy, dx):
        return ((y + dy) % NY) * 2 + (x + dx) % 2

    up, down, pair, sibling = at(dy=1), at(dy=3), at(dx=1), at(dc=1)
    far = {"dp_1": (xh + 1) % 2, "tensor_1": other_x}

    barrier = pltpu.get_barrier_semaphore()
    peers = [at(dy=dy, dx=dx) for dy in range(4) for dx in range(2) if dy or dx]
    peers += [sibling, at(dx=1, dc=1), far]

    def greet(sem_up, sem_down, distance):
        @pl.when(z + distance < NZ)
        def _():
            pl.semaphore_signal(sem_up, inc=1, device_id={"dp_0": (z + distance) % NZ}, device_id_type=MESH)

        @pl.when(z >= distance)
        def _():
            pl.semaphore_signal(sem_down, inc=1, device_id={"dp_0": (z + NZ - distance) % NZ}, device_id_type=MESH)

    def greet_round(r):
        greet(chain.at[2 * r], chain.at[2 * r + 1], 2 ** r)

    def greeted_round(r):
        distance = 2 ** r

        @pl.when(z >= distance)
        def _():
            pl.semaphore_wait(chain.at[2 * r], 1)

        @pl.when(z + distance < NZ)
        def _():
            pl.semaphore_wait(chain.at[2 * r + 1], 1)

    for peer in peers:
        pl.semaphore_signal(barrier, inc=1, device_id=peer, device_id_type=MESH)
    greet(barrier, barrier, 1)

    contract_last = (((1,), (1,)), ((), ()))
    loads = {}

    def load(name, src, dst, sem):
        loads[name] = pltpu.make_async_copy(src, dst, sem)
        loads[name].start()

    my_wk = wkfull.at[pl.ds(mult(c * 64, 64), 64), :]
    for k, (name, src, dst) in enumerate((
        ("tok", tokens, tok), ("gain", gain_in, gain_v), ("bkv", bkv_in, bkv_v), ("wk", wkv, my_wk),
        ("bq", bq_in, bq_v), ("weights", weights, weights_v), ("wq", wq, wqv), ("cos", cos, cosv), ("sin", sin, sinv),
    )):
        load(name, src, dst, ld.at[k])
    my_wo = pl.ds(mult(slot * QCOLS, QCOLS), QCOLS)
    for j in range(CHUNKS):
        pltpu.make_async_copy(wo.at[:, pl.ds(j * CW, CW)], wo4.at[j, my_wo, :], ld.at[9]).start()

    def send(src, dst, group, rsem, device):
        copy = pltpu.make_async_remote_copy(
            src_ref=src, dst_ref=dst, send_sem=sent.at[group], recv_sem=rsem,
            device_id=device, device_id_type=MESH,
        )
        copy.start()

    def all_sent(group, size):
        pltpu.make_async_remote_copy(
            src_ref=size, dst_ref=size, send_sem=sent.at[group], recv_sem=agr.at[0],
            device_id=sibling, device_id_type=MESH,
        ).wait_send()

    def arrived(dst, rsem):
        pltpu.make_async_remote_copy(
            src_ref=dst, dst_ref=dst, send_sem=sent.at[0], recv_sem=rsem,
            device_id=sibling, device_id_type=MESH,
        ).wait_recv()

    base = (y * 4 + slot) * ROWS
    loads["tok"].wait()
    loads["gain"].wait()
    gain = gain_v[...].astype(F32).reshape(1, D)
    for q in range(4):
        part = tok[q * QUARTER:(q + 1) * QUARTER, :].astype(F32)
        mean = jnp.mean(part * part, axis=-1, keepdims=True)
        xg[pl.ds(mult(base + q * QUARTER, QUARTER), QUARTER), :] = (
            part * lax.rsqrt(mean + EPS) * gain
        ).astype(BF16)

    pl.semaphore_wait(barrier, len(peers) + (z + NZ - 1) // NZ + (2 * NZ - 2 - z) // NZ)
    greet_round(0)

    def piece(u, q):
        return xg.at[pl.ds(mult(u * 128 + c * ROWS + q * QUARTER, QUARTER), QUARTER), :]

    def sibling_piece(u, q):
        return xg.at[pl.ds(mult(u * 128 + other_c * ROWS + q * QUARTER, QUARTER), QUARTER), :]

    def relay(u, q, device):
        send(piece(u, q), piece(u, q), GATHER, agr.at[u * 4 + q], device)

    def relay_sibling(u, q):
        send(piece(u, q), piece(u, q), SIBLING, agd.at[u], sibling)

    def wait_piece(u, q):
        arrived(piece(u, q), agr.at[u * 4 + q])

    def wait_sibling(u):
        arrived(xg.at[plane_rows(u, other_c), :], agd.at[u])

    def plane_rows(u, plane):
        return pl.ds(mult(u * 128 + plane * ROWS, ROWS), ROWS)

    own = unit(0, 0)
    for s in range(4):
        relay(own, s, up)
        relay(own, (s + 2) % 4, down)
        relay(own, s, pair)
    for q in range(4):
        relay_sibling(own, q)

    loads["wk"].wait()
    send(my_wk, my_wk, SIBLING_WK, wkr.at[0], sibling)
    loads["bkv"].wait()
    bias_mine = bkv_v[...].astype(F32).reshape(1, 64)
    bias_mine = jnp.concatenate([bias_mine, bias_mine], axis=1)
    bmine[...] = jnp.broadcast_to(bias_mine, (8, 128))
    send(bmine, bpair, SIBLING_BIAS, wkr.at[1], sibling)

    def wo_piece(j, owner):
        return wo4.at[j, pl.ds(mult(owner * QCOLS, QCOLS), QCOLS), :]

    pltpu.make_async_copy(wo4.at[:, my_wo, :], wo4.at[:, my_wo, :], ld.at[9]).wait()
    for j in range(CHUNKS):
        route = pair if j == NEAR_CHUNK else far
        send(wo_piece(j, slot), wo_piece(j, slot), WO, wor.at[j], route)
        send(wo_piece(j, slot), wo_piece(j, slot), WO_SIBLING, wod.at[CHUNKS], sibling)

    far_slot = other_x * 2 + c
    sibling_slot = x * 2 + other_c
    far_sibling_slot = other_x * 2 + other_c

    def forward_wo(j):
        arrived(wo_piece(j, far_slot), wor.at[j])
        send(wo_piece(j, far_slot), wo_piece(j, far_slot), WO_SIBLING, wod.at[j], sibling)

    arrived(wkfull.at[pl.ds(mult(other_c * 64, 64), 64), :], wkr.at[0])
    arrived(bpair, wkr.at[1])
    first = c == 0
    lane = lax.broadcasted_iota(jnp.int32, (1, 128), 1)
    bias_theirs = bpair[0:1, :]
    low_half = lane < 64
    kv_bias = jnp.where(
        first,
        jnp.where(low_half, bias_mine, bias_theirs),
        jnp.where(low_half, bias_theirs, bias_mine),
    )
    loads["bq"].wait()
    q_bias = bq_v[...].astype(F32).reshape(1, QCOLS)
    loads["wq"].wait()
    loads["cos"].wait()
    loads["sin"].wait()

    chip = y * 2 + x
    is_value = y // 2
    turned = (1 - is_value).astype(F32)
    straight = is_value.astype(F32)
    group = chip % NY
    local_user = group == y

    def rope(value, cosine, sine):
        return value * cosine + pltpu.roll(value, 64, 1) * sine

    def push(step, rows_kv, group, sem, device):
        return pltpu.make_async_remote_copy(
            src_ref=kvs.at[step], dst_ref=kv.at[is_value, rows_kv, :],
            send_sem=sent.at[group], recv_sem=sem, device_id=device, device_id_type=MESH,
        )

    def make_pairs(steps, units):
        lhs = [xg[plane_rows(u, c), :] for u in units]
        lhs = lhs[0] if len(lhs) == 1 else jnp.concatenate(lhs, axis=0)
        made_rows = lax.dot_general(
            lhs, wkfull[...], contract_last, preferred_element_type=F32
        ) + kv_bias
        made_rows = made_rows.astype(BF16).astype(F32)
        for i, (step, u) in enumerate(zip(steps, units)):
            rows_kv = plane_rows(u, c)
            cosine = cosv[rows_kv, :] * turned + straight
            sine = sinv[rows_kv, :] * turned
            result = rope(made_rows[i * ROWS:(i + 1) * ROWS, :], cosine, sine).astype(BF16)
            kvs[step] = result
            late = step >= LATE
            sem = kvr.at[is_value + (2 if late else 0)]

            @pl.when(local_user)
            def _():
                kv[is_value, rows_kv, :] = result

            @pl.when(jnp.logical_not(local_user))
            def _():
                push(step, rows_kv, MADE_HERE, sem, {"tensor_0": group}).start()

            push(step, rows_kv, MADE, sem, {"tensor_0": group, "tensor_1": other_x}).start()
            if late:
                for px in (other_x, x):
                    push(
                        step, rows_kv, MADE, kvd, {"tensor_0": group, "tensor_1": px, "tensor_2": other_c}
                    ).start()

    def make_query(units):
        lhs = [xg[pl.ds(mult(u * 128, 128), 128), :] for u in units]
        lhs = lhs[0] if len(lhs) == 1 else jnp.concatenate(lhs, axis=0)
        query = jnp.dot(lhs, wqv[...], preferred_element_type=F32) + q_bias
        for i, u in enumerate(units):
            rows = pl.ds(mult(u * 128, 128), 128)
            for h in range(2):
                cols = slice(h * HD, (h + 1) * HD)
                part = query[i * 128:(i + 1) * 128, cols]
                qb[rows, cols] = rope(part, cosv[rows, :], sinv[rows, :]).astype(BF16)

    def project(step, u):
        wait_sibling(u)
        make_pairs([step], [u])
        make_query([u])

    below, above, beside, across = unit(3, 0), unit(1, 0), unit(0, 1), unit(2, 0)
    x_across, x_below, x_above = unit(2, 1), unit(3, 1), unit(1, 1)

    greeted_round(0)
    greet_round(1)
    project(0, own)
    for s in range(4):
        wait_piece(below, s)
        if s < 2:
            relay(below, s, up)
        r = (s + 2) % 4
        wait_piece(above, r)
        if s < 2:
            relay(above, r, down)
        wait_piece(beside, s)
        relay(beside, s, up)
        relay(beside, s, down)
        relay_sibling(below, s)
        relay_sibling(above, r)
        relay_sibling(beside, s)
    greeted_round(1)
    greet_round(2)
    project(1, below)
    for q in (0, 2):
        wait_piece(across, q)
        relay(across, q, pair)
        relay_sibling(across, q)
    forward_wo(0)
    project(2, above)
    for u in (x_below, x_above):
        wait_piece(u, 0)
        relay_sibling(u, 0)
    forward_wo(1)
    project(3, beside)
    for q in (1, 3):
        wait_piece(across, q)
        relay(across, q, pair)
        relay_sibling(across, q)
    for q in (0, 2):
        wait_piece(x_across, q)
        relay_sibling(x_across, q)
    for u in (x_below, x_above):
        wait_piece(u, 1)
        relay_sibling(u, 1)
    greeted_round(2)
    project(4, across)
    forward_wo(2)
    for u in (x_below, x_above):
        wait_piece(u, 2)
        relay_sibling(u, 2)
    for q in (1, 3):
        wait_piece(x_across, q)
        relay_sibling(x_across, q)
    make_pairs([5], [x_across])
    for u in (x_below, x_above):
        wait_piece(u, 3)
        relay_sibling(u, 3)
    make_pairs([6, 7], [x_below, x_above])

    made_here = [
        jnp.logical_and(y == 0, x == 0),
        jnp.logical_and(y == 3, x == 1),
    ]
    order = ((0, 0), (3, 0), (1, 0), (0, 1), (2, 0), (2, 1), (3, 1), (1, 1))

    def source_unit(kind, step):
        dy, dx = order[step]
        return ((kind * 2 + y // 2 + dy) % NY) * 2 + (y % 2 + dx) % 2

    def wait_made(kind, steps, late):
        @pl.when(jnp.logical_not(made_here[kind]))
        def _():
            arrived(kv.at[kind, 0:steps * ROWS, :], kvr.at[kind + 2 * late])

    def forward_made(kind):
        wait_made(kind, LATE, 0)
        for step in range(LATE):
            part = kv.at[kind, plane_rows(source_unit(kind, step), c), :]
            send(part, part, MADE_SIBLING, kvd, sibling)

    wait_sibling(x_across)
    make_query([x_across])
    forward_wo(3)
    wait_sibling(x_below)
    wait_sibling(x_above)
    make_query([x_below, x_above])
    for kind in range(2):
        forward_made(kind)
    for kind in range(2):
        wait_made(kind, 8 - LATE, 1)
    arrived(kv.at[0], kvd)

    scale = HD ** (-0.5)
    my_cols = pl.ds(mult(slot * QCOLS, QCOLS), QCOLS)
    beyond = ((1, 0), (1, 1), (0, 1))

    def theirs(dx, dc):
        return ((x + dx) % 2) * 2 + (c + dc) % 2

    def block_attention(v):
        block, before = slice(v * 256, (v + 1) * 256), slice(0, v * 256)
        row = lax.broadcasted_iota(jnp.int32, (256, 256), 0)
        col = lax.broadcasted_iota(jnp.int32, (256, 256), 1)
        for h in range(2):
            cols = slice(h * HD, (h + 1) * HD)
            query = qb[block, cols]
            diagonal = lax.dot_general(query, kv[0, block, :], contract_last, preferred_element_type=F32)
            diagonal = jnp.where(row >= col, diagonal, -1e30)
            top = jnp.max(diagonal, axis=-1, keepdims=True)
            if v:
                earlier = lax.dot_general(query, kv[0, before, :], contract_last, preferred_element_type=F32)
                top = jnp.maximum(top, jnp.max(earlier, axis=-1, keepdims=True))
            weight = jnp.exp((diagonal - top) * scale)
            total = jnp.sum(weight, axis=-1, keepdims=True)
            mixed = jnp.dot(weight.astype(BF16), kv[1, block, :], preferred_element_type=F32)
            if v:
                weight = jnp.exp((earlier - top) * scale)
                total += jnp.sum(weight, axis=-1, keepdims=True)
                mixed += jnp.dot(weight.astype(BF16), kv[1, before, :], preferred_element_type=F32)
            ctx[block, cols] = (mixed / total).astype(BF16)

    def attend(k):
        b = (y + (2, 1, 3, 0)[k]) % NY
        for v in range(NY):
            @pl.when(b == v)
            def _(v=v):
                block_attention(v)

        target = pl.ds(k * ROWS, ROWS)
        ctx4[target, my_cols] = ctx[pl.ds(mult(b * 256 + slot * ROWS, ROWS), ROWS), :]
        for i, (dx, dc) in enumerate(beyond):
            send(
                ctx.at[pl.ds(mult(b * 256 + theirs(dx, dc) * ROWS, ROWS), ROWS), :],
                ctx4.at[target, my_cols],
                CONTEXT, cxr.at[k], at(dx=dx, dc=dc),
            )

    def gathered(k):
        arrived(ctx.at[0:3 * ROWS, :], cxr.at[k])

    def line(axis, index, size):
        return [{axis: (index + d) % size} for d in range(1, size)]

    cross = [
        {"dp_1": (xh + dh) % 2, "tensor_1": (x + dx) % 2, "tensor_2": (c + dc) % 2}
        for dh in range(2) for dx in range(2) for dc in range(2) if dh or dx or dc
    ]
    stages = [
        (line("tensor_0", y, NY), cy, y),
        (line("dp_0", z, NZ), cz, z),
        (cross, cc, xh * 4 + slot),
    ]

    def stage_start(i):
        devices, buf, index = stages[i]
        for device in devices:
            send(buf.at[index], buf.at[index], CHECK, cdr.at[i], device)

    def stage_end(i):
        devices, buf, _ = stages[i]
        arrived(buf.at[0:len(devices)], cdr.at[i])
        total = buf[0]
        for k in range(1, len(devices) + 1):
            total = total + buf[k]
        if i + 1 < len(stages):
            stages[i + 1][1][stages[i + 1][2]] = total
        else:
            total = total * (1.0 / 128.0)
            for j in range(CHUNKS):
                check_v[0:1, j * CW:(j + 1) * CW] = total[j:j + 1, :]
            pltpu.make_async_copy(check_v, check, stored.at[1]).start()

    attend(0)
    forward_wo(4)
    attend(1)
    forward_wo(5)
    forward_wo(NEAR_CHUNK)
    attend(2)
    attend(3)

    loads["weights"].wait()
    summary = jnp.dot(split3(weights_v[...]), ctx[...], preferred_element_type=F32)
    summary = split3(jnp.sum(summary, axis=0, keepdims=True))
    for j in range(CHUNKS):
        term = jnp.dot(summary, wo4[j, my_cols, :], preferred_element_type=F32)
        cy[y, j:j + 1, :] = jnp.sum(term, axis=0, keepdims=True)
    stage_start(0)
    gathered(0)

    far_rows, up_rows, down_rows, own_rows = (slice(k * ROWS, (k + 1) * ROWS) for k in range(4))
    arrived(wo4.at[:, pl.ds(mult(sibling_slot * QCOLS, QCOLS), QCOLS), :], wod.at[CHUNKS])
    for j in range(CHUNKS):
        if j == 4:
            forward_wo(6)
        arrived(wo_piece(j, far_sibling_slot), wod.at[j])
        product = jnp.dot(ctx4[far_rows, :], wo4[j], preferred_element_type=F32)
        pbuf[j, far_rows, :] = product.astype(BF16)
        send(pbuf.at[j, far_rows, :], ra.at[j], SUM, rar.at[j], down if j % 2 else up)

    stage_end(0)
    stage_start(1)
    for k in range(1, 4):
        gathered(k)
    for j in range(CHUNKS):
        product = jnp.dot(ctx4[ROWS:256, :], wo4[j], preferred_element_type=F32)
        pbuf[j, ROWS:256, :] = product.astype(BF16)
        if j % 2 == 0:
            send(pbuf.at[j, down_rows, :], rfa.at[j], SUM, rtr.at[j], down)
        else:
            send(pbuf.at[j, up_rows, :], rfb.at[j], SUM, rbr.at[j], up)

    for j in range(CHUNKS):
        rows = up_rows if j % 2 == 0 else down_rows
        arrived(ra.at[j], rar.at[j])
        pbuf[j, rows, :] = (pbuf[j, rows, :].astype(F32) + ra[j].astype(F32)).astype(BF16)
        if j % 2 == 0:
            send(pbuf.at[j, rows, :], rfb.at[j], SUM, rbr.at[j], up)
        else:
            send(pbuf.at[j, rows, :], rfa.at[j], SUM, rtr.at[j], down)
    stage_end(1)
    stage_start(2)
    stage_end(2)

    for j in (1, 3, 5, 7, 0, 2, 4, 6):
        arrived(rfb.at[j], rbr.at[j])
        arrived(rfa.at[j], rtr.at[j])
        total = pbuf[j, own_rows, :].astype(F32) + rfb[j].astype(F32) + rfa[j].astype(F32)
        cols = slice(j * CW, (j + 1) * CW)
        outv[:, cols] = total.astype(BF16)
        pltpu.make_async_copy(outv.at[:, cols], out.at[:, cols], stored.at[0]).start()

    all_sent(GATHER, xg.at[0:28 * QUARTER, :])
    all_sent(SIBLING, xg.at[0:32 * QUARTER, :])
    all_sent(SIBLING_WK, my_wk)
    all_sent(SIBLING_BIAS, bmine)
    all_sent(WO, wo4.at[:, 0:QCOLS, :])
    all_sent(WO_SIBLING, wo4.at[:, 0:2 * QCOLS, :])
    all_sent(MADE, kv.at[0, 0:14 * ROWS, :])
    all_sent(MADE_SIBLING, kv.at[:, 0:LATE * ROWS, :])
    all_sent(CONTEXT, ctx.at[0:12 * ROWS, :])
    all_sent(SUM, xg.at[0:192, :])
    all_sent(CHECK, wo4.at[0, 0:17 * 16, :])

    @pl.when(jnp.logical_not(local_user))
    def _():
        all_sent(MADE_HERE, kv.at[0, 0:8 * ROWS, :])

    pltpu.make_async_copy(outv, out, stored.at[0]).wait()
    pltpu.make_async_copy(check_v, check, stored.at[1]).wait()


def tables():
    half = HD // 2
    inverse = THETA ** (-(np.arange(half, dtype=np.float64) * 2.0 / HD))
    angles = np.arange(SEQ, dtype=np.float64)[:, None] * inverse[None, :]
    cosine, sine = np.cos(angles), np.sin(angles)
    return (
        np.concatenate([cosine, cosine], axis=1).astype(np.float32),
        np.concatenate([-sine, sine], axis=1).astype(np.float32),
    )


def local(tokens, gain, wq, bq, wkv, bkv, wo, check_weights):
    cosine, sine = tables()
    dma = pltpu.SemaphoreType.DMA
    vmem = pltpu.VMEM
    anywhere = pl.BlockSpec(memory_space=pl.ANY)
    attended, total = pl.pallas_call(
        kernel,
        out_shape=(
            jax.ShapeDtypeStruct((ROWS, D), BF16),
            jax.ShapeDtypeStruct((1, D), F32),
        ),
        in_specs=[anywhere] * 10,
        out_specs=(anywhere, anywhere),
        scratch_shapes=[
            vmem((ROWS, D), BF16),
            vmem((D,), BF16),
            vmem((QCOLS,), BF16),
            vmem((64,), BF16),
            vmem((1, SEQ), F32),
            vmem((1, D), F32),
            vmem((SEQ, D), BF16),
            vmem((D, QCOLS), BF16),
            vmem((128, D), BF16),
            vmem((8, 128), F32),
            vmem((8, 128), F32),
            vmem((SEQ, HD), F32),
            vmem((SEQ, HD), F32),
            vmem((SEQ, QCOLS), BF16),
            vmem((8, ROWS, HD), BF16),
            vmem((2, SEQ, HD), BF16),
            vmem((SEQ, QCOLS), BF16),
            vmem((256, SEQ), BF16),
            vmem((CHUNKS, SEQ, CW), BF16),
            vmem((CHUNKS, 256, CW), BF16),
            vmem((CHUNKS, ROWS, CW), BF16),
            vmem((CHUNKS, ROWS, CW), BF16),
            vmem((CHUNKS, ROWS, CW), BF16),
            vmem((ROWS, D), BF16),
            vmem((NY, CHUNKS, CW), F32),
            vmem((NZ, CHUNKS, CW), F32),
            vmem((8, CHUNKS, CW), F32),
            dma((10,)), dma((32,)), dma((8,)), dma((2,)), dma((CHUNKS,)), dma((CHUNKS + 1,)),
            dma((4,)), dma, dma((4,)), dma((CHUNKS,)), dma((CHUNKS,)), dma((CHUNKS,)),
            dma((3,)), dma((12,)), dma((2,)), pltpu.SemaphoreType.REGULAR((6,)),
        ],
        compiler_params=pltpu.CompilerParams(
            collective_id=0, has_side_effects=True, vmem_limit_bytes=56 * 1024 * 1024
        ),
        name="sublayer",
    )(tokens[0], gain, bq, bkv, wq, wkv.T, wo, check_weights, cosine, sine)
    return attended[None], total.reshape(D)


def solution(mesh):
    torus = Mesh(
        mesh.devices.reshape(8, 2, 4, 2, 2), ("dp_0", "dp_1", "tensor_0", "tensor_1", "tensor_2")
    )
    return jax.shard_map(
        local,
        mesh=torus,
        in_specs=(
            P(DP, TENSOR, None),
            P(),
            P(None, TENSOR),
            P(TENSOR),
            P(None, TENSOR),
            P(TENSOR),
            P(TENSOR, None),
            P(DP, None),
        ),
        out_specs=(P(DP, TENSOR, None), P()),
        check_vma=False,
    )
```

time: 83.4 us -> 72.6 us (0.87)
  the two profiles are of different devices: /device:TPU:4 before, /device:TPU:1 now
where the time goes in v3:
time: 72.6 us; the launch traced here: 72.4 us
  Pallas kernels  68.6 us (94%)
  local copies, waits for them, and re-layouts  3.19 us (4%)
    pallas_call x1, Pallas kernels, local(): pl.pallas_call(kernel, out_shape=(jax.ShapeDtypeStruct((ROWS, D), BF16),...  68.6 us
    unnamed x2, local copies, waits for them, and re-layouts  3.19 us

profile of v3, /device:TPU:1, one launch (start us, length us, event | category | flops | bytes accessed | tf_op | source)
XLA Modules:
  0.0 72.4 jit_solution(5923321889555433187)
XLA Ops:
  0.6 68.6 %sublayer.1 = (bf16[64,4096]{1,0:T(8,128)(2,1)}, f32[1,4096]{1,0:T(1,128)}) custom-call(bf16[64,4096]{1,0:T(8,128)(2,1)} %bitcast.4, bf16[4096]{0:T(1024)(128)(2,1)} %gain_in.1, bf16[256]{0:T(256)(128)(2,1)} %bq_in.1, bf16[64]{0:T(256)(128)(2,1)} %bkv_in.1, bf16[4096,256]{1,0:T(8,128)(2,1)} %wq.1, bf16[64,4096]{1,0:T(8,128)(2,1)} %bitcast.5, ...), custom_call_target="tpu_custom_call" | custom-call | tf_op jit(solution)/shard_map/sublayer/pallas_call | solution.py:556
  69.2 1.9 %copy.14 = bf16[1,64,4096]{2,1,0:T(8,128)(2,1)} copy(bf16[1,64,4096]{2,1,0:T(8,128)(2,1)} %bitcast.6) | data formatting | bytes 1048576
  71.1 1.3 %copy.15 = f32[4096]{0:T(1024)} copy(f32[4096]{0:T(1024)} %bitcast.7) | data formatting | bytes 32768

commit v4 on v3

--- a/solution.py
+++ b/solution.py
@@ -25,8 +25,9 @@
 SEQ = 1024
 CHUNKS = 8
 CW = D // CHUNKS
+LATE = 4
 NEAR_CHUNK = 7
-LATE = 5
+LAST_CHUNK = 6
 (
     GATHER, SIBLING, SIBLING_WK, SIBLING_BIAS, WO, WO_SIBLING, MADE, MADE_HERE, MADE_SIBLING, CONTEXT, SUM, CHECK,
 ) = range(12)
@@ -49,9 +50,9 @@
 def kernel(
     tokens, gain_in, bq_in, bkv_in, wq, wkv, wo, weights, cos, sin,
     out, check,
-    tok, gain_v, bq_v, bkv_v, weights_v, check_v, xg, wqv, wkfull, bmine, bpair, cosv, sinv, qb, kvs, kv,
-    ctx, ctx4, wo4, pbuf, ra, rfb, rfa, outv, cy, cz, cc,
-    ld, agr, agd, wkr, wor, wod, kvr, kvd, cxr, rar, rbr, rtr, cdr, sent, stored, chain,
+    tok, gain_v, bq_v, bkv_v, weights_v, xg, wqv, wkfull, wkt, bmine, bpair, cosv, sinv, qb, kvs, kv,
+    ctx, ctx4, wo4, pbuf, ra, rfb, rfa, cy, cz, cc,
+    ld, agr, agx, agd, wkr, wor, wod, kvr, kvd, cxr, rar, rbr, rtr, cdr, sent, chain,
 ):
     z = lax.axis_index("dp_0")
     xh = lax.axis_index("dp_1")
@@ -167,6 +168,13 @@
     def wait_piece(u, q):
         arrived(piece(u, q), agr.at[u * 4 + q])
 
+    def half_piece(u, q, side):
+        rows = pl.ds(mult(u * 128 + c * ROWS + q * QUARTER, QUARTER), QUARTER)
+        return xg.at[rows, side * (D // 2):(side + 1) * (D // 2)]
+
+    def relay_half(u, q, side, sem, device):
+        send(half_piece(u, q, side), half_piece(u, q, side), GATHER, sem, device)
+
     def wait_sibling(u):
         arrived(xg.at[plane_rows(u, other_c), :], agd.at[u])
 
@@ -175,8 +183,9 @@
 
     own = unit(0, 0)
     for s in range(4):
-        relay(own, s, up)
-        relay(own, (s + 2) % 4, down)
+        if s < 3:
+            relay(own, s, up)
+            relay(own, (s + 2) % 4, down)
         relay(own, s, pair)
     for q in range(4):
         relay_sibling(own, q)
@@ -194,9 +203,13 @@
 
     pltpu.make_async_copy(wo4.at[:, my_wo, :], wo4.at[:, my_wo, :], ld.at[9]).wait()
     for j in range(CHUNKS):
-        route = pair if j == NEAR_CHUNK else far
-        send(wo_piece(j, slot), wo_piece(j, slot), WO, wor.at[j], route)
+        if j != NEAR_CHUNK:
+            send(wo_piece(j, slot), wo_piece(j, slot), WO, wor.at[j], far)
         send(wo_piece(j, slot), wo_piece(j, slot), WO_SIBLING, wod.at[CHUNKS], sibling)
+
+    def send_near_chunk(half):
+        part = wo4.at[NEAR_CHUNK, pl.ds(mult(slot * QCOLS + half * 128, 128), 128), :]
+        send(part, part, WO, wor.at[NEAR_CHUNK], pair)
 
     far_slot = other_x * 2 + c
     sibling_slot = x * 2 + other_c
@@ -208,6 +221,9 @@
 
     arrived(wkfull.at[pl.ds(mult(other_c * 64, 64), 64), :], wkr.at[0])
     arrived(bpair, wkr.at[1])
+    for i in range(8):
+        cols = slice(i * 512, (i + 1) * 512)
+        wkt[cols, :] = wkfull[:, cols].T
     first = c == 0
     lane = lax.broadcasted_iota(jnp.int32, (1, 128), 1)
     bias_theirs = bpair[0:1, :]
@@ -242,9 +258,7 @@
     def make_pairs(steps, units):
         lhs = [xg[plane_rows(u, c), :] for u in units]
         lhs = lhs[0] if len(lhs) == 1 else jnp.concatenate(lhs, axis=0)
-        made_rows = lax.dot_general(
-            lhs, wkfull[...], contract_last, preferred_element_type=F32
-        ) + kv_bias
+        made_rows = jnp.dot(lhs, wkt[...], preferred_element_type=F32) + kv_bias
         made_rows = made_rows.astype(BF16).astype(F32)
         for i, (step, u) in enumerate(zip(steps, units)):
             rows_kv = plane_rows(u, c)
@@ -292,58 +306,75 @@
     greeted_round(0)
     greet_round(1)
     project(0, own)
+    def relay_across(*quarters):
+        for q in quarters:
+            wait_piece(across, q)
+            relay(across, q, pair)
+            relay_sibling(across, q)
+
+    def relay_beside(q):
+        for device, halved in ((up, 0), (down, 2)):
+            if q == halved:
+                relay_half(beside, q, 0, agr.at[beside * 4 + q], device)
+            else:
+                relay(beside, q, device)
+
     for s in range(4):
+        if s == 3:
+            relay_across(0, 2)
+        r = (s + 2) % 4
         wait_piece(below, s)
+        wait_piece(above, r)
         if s < 2:
             relay(below, s, up)
-        r = (s + 2) % 4
-        wait_piece(above, r)
-        if s < 2:
             relay(above, r, down)
+        if s == 0:
+            relay(own, 3, up)
+            relay(own, 1, down)
+            relay_half(below, s, 1, agx.at[0], pair)
+            relay_half(above, r, 1, agx.at[1], pair)
         wait_piece(beside, s)
-        relay(beside, s, up)
-        relay(beside, s, down)
+        for q in ((), (0, 1), (2,), (3,))[s]:
+            relay_beside(q)
         relay_sibling(below, s)
         relay_sibling(above, r)
         relay_sibling(beside, s)
     greeted_round(1)
     greet_round(2)
+
+    def wait_x_neighbours(q):
+        for k, (u, halved) in enumerate(((x_below, 0), (x_above, 2))):
+            if q == halved:
+                arrived(half_piece(u, q, 0), agr.at[u * 4 + q])
+                arrived(half_piece(u, q, 1), agx.at[k])
+            else:
+                wait_piece(u, q)
+            relay_sibling(u, q)
+
+    def wait_x_across(*quarters):
+        for q in quarters:
+            wait_piece(x_across, q)
+            relay_sibling(x_across, q)
+
     project(1, below)
-    for q in (0, 2):
-        wait_piece(across, q)
-        relay(across, q, pair)
-        relay_sibling(across, q)
+    relay_across(1, 3)
+    send_near_chunk(0)
+    project(2, above)
     forward_wo(0)
-    project(2, above)
-    for u in (x_below, x_above):
-        wait_piece(u, 0)
-        relay_sibling(u, 0)
+    project(3, beside)
+    wait_x_neighbours(0)
     forward_wo(1)
-    project(3, beside)
-    for q in (1, 3):
-        wait_piece(across, q)
-        relay(across, q, pair)
-        relay_sibling(across, q)
-    for q in (0, 2):
-        wait_piece(x_across, q)
-        relay_sibling(x_across, q)
-    for u in (x_below, x_above):
-        wait_piece(u, 1)
-        relay_sibling(u, 1)
+    wait_x_across(0, 2)
+    wait_x_neighbours(1)
     greeted_round(2)
     project(4, across)
     forward_wo(2)
-    for u in (x_below, x_above):
-        wait_piece(u, 2)
-        relay_sibling(u, 2)
-    for q in (1, 3):
-        wait_piece(x_across, q)
-        relay_sibling(x_across, q)
+    wait_x_neighbours(2)
+    wait_x_across(1, 3)
     make_pairs([5], [x_across])
-    for u in (x_below, x_above):
-        wait_piece(u, 3)
-        relay_sibling(u, 3)
+    wait_x_neighbours(3)
     make_pairs([6, 7], [x_below, x_above])
+    send_near_chunk(1)
 
     made_here = [
         jnp.logical_and(y == 0, x == 0),
@@ -366,6 +397,8 @@
             part = kv.at[kind, plane_rows(source_unit(kind, step), c), :]
             send(part, part, MADE_SIBLING, kvd, sibling)
 
+    for kind in range(2):
+        forward_made(kind)
     wait_sibling(x_across)
     make_query([x_across])
     forward_wo(3)
@@ -373,8 +406,6 @@
     wait_sibling(x_above)
     make_query([x_below, x_above])
     for kind in range(2):
-        forward_made(kind)
-    for kind in range(2):
         wait_made(kind, 8 - LATE, 1)
     arrived(kv.at[0], kvd)
 
@@ -385,43 +416,45 @@
     def theirs(dx, dc):
         return ((x + dx) % 2) * 2 + (c + dc) % 2
 
-    def block_attention(v):
+    def head_attention(v, h):
         block, before = slice(v * 256, (v + 1) * 256), slice(0, v * 256)
         row = lax.broadcasted_iota(jnp.int32, (256, 256), 0)
         col = lax.broadcasted_iota(jnp.int32, (256, 256), 1)
-        for h in range(2):
-            cols = slice(h * HD, (h + 1) * HD)
-            query = qb[block, cols]
-            diagonal = lax.dot_general(query, kv[0, block, :], contract_last, preferred_element_type=F32)
-            diagonal = jnp.where(row >= col, diagonal, -1e30)
-            top = jnp.max(diagonal, axis=-1, keepdims=True)
-            if v:
-                earlier = lax.dot_general(query, kv[0, before, :], contract_last, preferred_element_type=F32)
-                top = jnp.maximum(top, jnp.max(earlier, axis=-1, keepdims=True))
-            weight = jnp.exp((diagonal - top) * scale)
-            total = jnp.sum(weight, axis=-1, keepdims=True)
-            mixed = jnp.dot(weight.astype(BF16), kv[1, block, :], preferred_element_type=F32)
-            if v:
-                weight = jnp.exp((earlier - top) * scale)
-                total += jnp.sum(weight, axis=-1, keepdims=True)
-                mixed += jnp.dot(weight.astype(BF16), kv[1, before, :], preferred_element_type=F32)
-            ctx[block, cols] = (mixed / total).astype(BF16)
+        cols = slice(h * HD, (h + 1) * HD)
+        query = qb[block, cols]
+        diagonal = lax.dot_general(query, kv[0, block, :], contract_last, preferred_element_type=F32)
+        diagonal = jnp.where(row >= col, diagonal, -1e30)
+        top = jnp.max(diagonal, axis=-1, keepdims=True)
+        if v:
+            earlier = lax.dot_general(query, kv[0, before, :], contract_last, preferred_element_type=F32)
+            top = jnp.maximum(top, jnp.max(earlier, axis=-1, keepdims=True))
+        weight = jnp.exp((diagonal - top) * scale)
+        total = jnp.sum(weight, axis=-1, keepdims=True)
+        mixed = jnp.dot(weight.astype(BF16), kv[1, block, :], preferred_element_type=F32)
+        if v:
+            weight = jnp.exp((earlier - top) * scale)
+            total += jnp.sum(weight, axis=-1, keepdims=True)
+            mixed += jnp.dot(weight.astype(BF16), kv[1, before, :], preferred_element_type=F32)
+        ctx[block, cols] = (mixed / total).astype(BF16)
 
     def attend(k):
         b = (y + (2, 1, 3, 0)[k]) % NY
-        for v in range(NY):
-            @pl.when(b == v)
-            def _(v=v):
-                block_attention(v)
-
         target = pl.ds(k * ROWS, ROWS)
+        for h in range(2):
+            for v in range(NY):
+                @pl.when(b == v)
+                def _(v=v, h=h):
+                    head_attention(v, h)
+
+            cols = slice(h * HD, (h + 1) * HD)
+            head = pl.ds(mult(slot * QCOLS + h * HD, HD), HD)
+            for dx, dc in beyond:
+                send(
+                    ctx.at[pl.ds(mult(b * 256 + theirs(dx, dc) * ROWS, ROWS), ROWS), cols],
+                    ctx4.at[target, head],
+                    CONTEXT, cxr.at[k], at(dx=dx, dc=dc),
+                )
         ctx4[target, my_cols] = ctx[pl.ds(mult(b * 256 + slot * ROWS, ROWS), ROWS), :]
-        for i, (dx, dc) in enumerate(beyond):
-            send(
-                ctx.at[pl.ds(mult(b * 256 + theirs(dx, dc) * ROWS, ROWS), ROWS), :],
-                ctx4.at[target, my_cols],
-                CONTEXT, cxr.at[k], at(dx=dx, dc=dc),
-            )
 
     def gathered(k):
         arrived(ctx.at[0:3 * ROWS, :], cxr.at[k])
@@ -455,15 +488,14 @@
         else:
             total = total * (1.0 / 128.0)
             for j in range(CHUNKS):
-                check_v[0:1, j * CW:(j + 1) * CW] = total[j:j + 1, :]
-            pltpu.make_async_copy(check_v, check, stored.at[1]).start()
+                check[0:1, j * CW:(j + 1) * CW] = total[j:j + 1, :]
 
     attend(0)
     forward_wo(4)
     attend(1)
     forward_wo(5)
+    attend(2)
     forward_wo(NEAR_CHUNK)
-    attend(2)
     attend(3)
 
     loads["weights"].wait()
@@ -477,19 +509,14 @@
 
     far_rows, up_rows, down_rows, own_rows = (slice(k * ROWS, (k + 1) * ROWS) for k in range(4))
     arrived(wo4.at[:, pl.ds(mult(sibling_slot * QCOLS, QCOLS), QCOLS), :], wod.at[CHUNKS])
-    for j in range(CHUNKS):
-        if j == 4:
-            forward_wo(6)
+
+    def far_target(j):
         arrived(wo_piece(j, far_sibling_slot), wod.at[j])
         product = jnp.dot(ctx4[far_rows, :], wo4[j], preferred_element_type=F32)
         pbuf[j, far_rows, :] = product.astype(BF16)
         send(pbuf.at[j, far_rows, :], ra.at[j], SUM, rar.at[j], down if j % 2 else up)
 
-    stage_end(0)
-    stage_start(1)
-    for k in range(1, 4):
-        gathered(k)
-    for j in range(CHUNKS):
+    def near_targets(j):
         product = jnp.dot(ctx4[ROWS:256, :], wo4[j], preferred_element_type=F32)
         pbuf[j, ROWS:256, :] = product.astype(BF16)
         if j % 2 == 0:
@@ -497,7 +524,7 @@
         else:
             send(pbuf.at[j, up_rows, :], rfb.at[j], SUM, rbr.at[j], up)
 
-    for j in range(CHUNKS):
+    def relay_sum(j):
         rows = up_rows if j % 2 == 0 else down_rows
         arrived(ra.at[j], rar.at[j])
         pbuf[j, rows, :] = (pbuf[j, rows, :].astype(F32) + ra[j].astype(F32)).astype(BF16)
@@ -505,17 +532,32 @@
             send(pbuf.at[j, rows, :], rfb.at[j], SUM, rbr.at[j], up)
         else:
             send(pbuf.at[j, rows, :], rfa.at[j], SUM, rtr.at[j], down)
+
+    early = [j for j in range(CHUNKS) if j != LAST_CHUNK]
+    for j in early:
+        far_target(j)
+    forward_wo(LAST_CHUNK)
+    for k in range(1, 4):
+        gathered(k)
+    for j in early:
+        near_targets(j)
+        if j == 1:
+            stage_end(0)
+            stage_start(1)
+    far_target(LAST_CHUNK)
+    near_targets(LAST_CHUNK)
+    for j in early + [LAST_CHUNK]:
+        relay_sum(j)
     stage_end(1)
     stage_start(2)
-    stage_end(2)
-
-    for j in (1, 3, 5, 7, 0, 2, 4, 6):
+    for j in early + [LAST_CHUNK]:
         arrived(rfb.at[j], rbr.at[j])
         arrived(rfa.at[j], rtr.at[j])
         total = pbuf[j, own_rows, :].astype(F32) + rfb[j].astype(F32) + rfa[j].astype(F32)
         cols = slice(j * CW, (j + 1) * CW)
-        outv[:, cols] = total.astype(BF16)
-        pltpu.make_async_copy(outv.at[:, cols], out.at[:, cols], stored.at[0]).start()
+        out[:, cols] = total.astype(BF16)
+
+    stage_end(2)
 
     all_sent(GATHER, xg.at[0:28 * QUARTER, :])
     all_sent(SIBLING, xg.at[0:32 * QUARTER, :])
@@ -523,7 +565,7 @@
     all_sent(SIBLING_BIAS, bmine)
     all_sent(WO, wo4.at[:, 0:QCOLS, :])
     all_sent(WO_SIBLING, wo4.at[:, 0:2 * QCOLS, :])
-    all_sent(MADE, kv.at[0, 0:14 * ROWS, :])
+    all_sent(MADE, kv.at[0, 0:(24 - 2 * LATE) * ROWS, :])
     all_sent(MADE_SIBLING, kv.at[:, 0:LATE * ROWS, :])
     all_sent(CONTEXT, ctx.at[0:12 * ROWS, :])
     all_sent(SUM, xg.at[0:192, :])
@@ -533,8 +575,13 @@
     def _():
         all_sent(MADE_HERE, kv.at[0, 0:8 * ROWS, :])
 
-    pltpu.make_async_copy(outv, out, stored.at[0]).wait()
-    pltpu.make_async_copy(check_v, check, stored.at[1]).wait()
+
+def store_results(attended, total, out, check, sem):
+    copies = (pltpu.make_async_copy(total, check, sem.at[1]), pltpu.make_async_copy(attended, out, sem.at[0]))
+    for copy in copies:
+        copy.start()
+    for copy in copies:
+        copy.wait()
 
 
 def tables():
@@ -553,24 +600,25 @@
     dma = pltpu.SemaphoreType.DMA
     vmem = pltpu.VMEM
     anywhere = pl.BlockSpec(memory_space=pl.ANY)
+    inside = pl.BlockSpec(memory_space=pltpu.VMEM)
     attended, total = pl.pallas_call(
         kernel,
         out_shape=(
-            jax.ShapeDtypeStruct((ROWS, D), BF16),
-            jax.ShapeDtypeStruct((1, D), F32),
+            pltpu.VMEM((ROWS, D), BF16),
+            pltpu.VMEM((1, D), F32),
         ),
         in_specs=[anywhere] * 10,
-        out_specs=(anywhere, anywhere),
+        out_specs=(inside, inside),
         scratch_shapes=[
             vmem((ROWS, D), BF16),
             vmem((D,), BF16),
             vmem((QCOLS,), BF16),
             vmem((64,), BF16),
             vmem((1, SEQ), F32),
-            vmem((1, D), F32),
             vmem((SEQ, D), BF16),
             vmem((D, QCOLS), BF16),
             vmem((128, D), BF16),
+            vmem((D, 128), BF16),
             vmem((8, 128), F32),
             vmem((8, 128), F32),
             vmem((SEQ, HD), F32),
@@ -585,19 +633,29 @@
             vmem((CHUNKS, ROWS, CW), BF16),
             vmem((CHUNKS, ROWS, CW), BF16),
             vmem((CHUNKS, ROWS, CW), BF16),
-            vmem((ROWS, D), BF16),
             vmem((NY, CHUNKS, CW), F32),
             vmem((NZ, CHUNKS, CW), F32),
             vmem((8, CHUNKS, CW), F32),
-            dma((10,)), dma((32,)), dma((8,)), dma((2,)), dma((CHUNKS,)), dma((CHUNKS + 1,)),
+            dma((10,)), dma((32,)), dma((2,)), dma((8,)), dma((2,)), dma((CHUNKS,)), dma((CHUNKS + 1,)),
             dma((4,)), dma, dma((4,)), dma((CHUNKS,)), dma((CHUNKS,)), dma((CHUNKS,)),
-            dma((3,)), dma((12,)), dma((2,)), pltpu.SemaphoreType.REGULAR((6,)),
+            dma((3,)), dma((12,)), pltpu.SemaphoreType.REGULAR((6,)),
         ],
         compiler_params=pltpu.CompilerParams(
             collective_id=0, has_side_effects=True, vmem_limit_bytes=56 * 1024 * 1024
         ),
         name="sublayer",
     )(tokens[0], gain, bq, bkv, wq, wkv.T, wo, check_weights, cosine, sine)
+    attended, total = pl.pallas_call(
+        store_results,
+        out_shape=(jax.ShapeDtypeStruct((ROWS, D), BF16), jax.ShapeDtypeStruct((1, D), F32)),
+        in_specs=[inside, inside],
+        out_specs=(anywhere, anywhere),
+        scratch_shapes=[dma((2,))],
+        name="store_results",
+    )(
+        pltpu.with_memory_space_constraint(attended, pltpu.VMEM),
+        pltpu.with_memory_space_constraint(total, pltpu.VMEM),
+    )
     return attended[None], total.reshape(D)
 
 

time: 72.6 us -> 69.1 us (0.952)
  local copies, waits for them, and re-layouts: 3.19 us -> 0 us
    unnamed x2 -> x0, local copies, waits for them, and re-layouts: 3.19 us -> none
    pallas_call x1 -> x2, Pallas kernels: 68.6 us -> 68.1 us  [the longest x1 67.2 us: local(): pl.pallas_call(kernel, out_shape=(pltpu.VMEM((ROWS, D), BF16), pltpu.VMEM...]
where the time goes in v4:
time: 69.1 us; the launch traced here: 68.9 us
  Pallas kernels  68.1 us (99%)
  between operations  0.82 us (1%)
    pallas_call x1, Pallas kernels, local(): pl.pallas_call(kernel, out_shape=(pltpu.VMEM((ROWS, D), BF16), pltpu.VMEM...  67.2 us

profile of v4, /device:TPU:1, one launch (start us, length us, event | category | flops | bytes accessed | tf_op | source)
XLA Modules:
  0.0 68.9 jit_solution(791218507608366843)
XLA Ops:
  0.6 67.2 %sublayer.1 = (bf16[64,4096]{1,0:T(8,128)(2,1)S(1)}, f32[1,4096]{1,0:T(1,128)S(1)}) custom-call(bf16[64,4096]{1,0:T(8,128)(2,1)} %bitcast.4, bf16[4096]{0:T(1024)(128)(2,1)} %gain_in.1, bf16[256]{0:T(256)(128)(2,1)} %bq_in.1, bf16[64]{0:T(256)(128)(2,1)} %bkv_in.1, bf16[4096,256]{1,0:T(8,128)(2,1)} %wq.1, bf16[64,4096]{1,0:T(8,128)(2,1)} %bitcast.5, ...), custom_call_target="tpu_custom_call" | custom-call | tf_op jit(solution)/shard_map/sublayer/pallas_call | solution.py:604
  67.9 0.8 %store_results.1 = (bf16[64,4096]{1,0:T(8,128)(2,1)}, f32[1,4096]{1,0:T(1,128)}) custom-call(bf16[64,4096]{1,0:T(8,128)(2,1)S(1)} %get-tuple-element.6.attended, f32[1,4096]{1,0:T(1,128)S(1)} %get-tuple-element.7.total), custom_call_target="tpu_custom_call" | custom-call | tf_op jit(solution)/shard_map/store_results/pallas_call | solution.py:648

commit v5 on v4

--- a/solution.py
+++ b/solution.py
@@ -27,7 +27,6 @@
 CW = D // CHUNKS
 LATE = 4
 NEAR_CHUNK = 7
-LAST_CHUNK = 6
 (
     GATHER, SIBLING, SIBLING_WK, SIBLING_BIAS, WO, WO_SIBLING, MADE, MADE_HERE, MADE_SIBLING, CONTEXT, SUM, CHECK,
 ) = range(12)
@@ -52,7 +51,7 @@
     out, check,
     tok, gain_v, bq_v, bkv_v, weights_v, xg, wqv, wkfull, wkt, bmine, bpair, cosv, sinv, qb, kvs, kv,
     ctx, ctx4, wo4, pbuf, ra, rfb, rfa, cy, cz, cc,
-    ld, agr, agx, agd, wkr, wor, wod, kvr, kvd, cxr, rar, rbr, rtr, cdr, sent, chain,
+    ld, agr, agd, wkr, wor, wod, kvr, kvd, cxr, rar, rbr, cdr, sent, chain,
 ):
     z = lax.axis_index("dp_0")
     xh = lax.axis_index("dp_1")
@@ -72,9 +71,18 @@
     up, down, pair, sibling = at(dy=1), at(dy=3), at(dx=1), at(dc=1)
     far = {"dp_1": (xh + 1) % 2, "tensor_1": other_x}
 
+    contract_last = (((1,), (1,)), ((), ()))
+    loads = {}
+
+    def load(name, src, dst, sem):
+        loads[name] = pltpu.make_async_copy(src, dst, sem)
+        loads[name].start()
+
+    load("tok", tokens, tok, ld.at[0])
+    load("gain", gain_in, gain_v, ld.at[1])
+
     barrier = pltpu.get_barrier_semaphore()
-    peers = [at(dy=dy, dx=dx) for dy in range(4) for dx in range(2) if dy or dx]
-    peers += [sibling, at(dx=1, dc=1), far]
+    peers = (up, down, pair, sibling, far)
 
     def greet(sem_up, sem_down, distance):
         @pl.when(z + distance < NZ)
@@ -103,19 +111,12 @@
         pl.semaphore_signal(barrier, inc=1, device_id=peer, device_id_type=MESH)
     greet(barrier, barrier, 1)
 
-    contract_last = (((1,), (1,)), ((), ()))
-    loads = {}
-
-    def load(name, src, dst, sem):
-        loads[name] = pltpu.make_async_copy(src, dst, sem)
-        loads[name].start()
-
     my_wk = wkfull.at[pl.ds(mult(c * 64, 64), 64), :]
     for k, (name, src, dst) in enumerate((
-        ("tok", tokens, tok), ("gain", gain_in, gain_v), ("bkv", bkv_in, bkv_v), ("wk", wkv, my_wk),
+        ("bkv", bkv_in, bkv_v), ("wk", wkv, my_wk),
         ("bq", bq_in, bq_v), ("weights", weights, weights_v), ("wq", wq, wqv), ("cos", cos, cosv), ("sin", sin, sinv),
     )):
-        load(name, src, dst, ld.at[k])
+        load(name, src, dst, ld.at[2 + k])
     my_wo = pl.ds(mult(slot * QCOLS, QCOLS), QCOLS)
     for j in range(CHUNKS):
         pltpu.make_async_copy(wo.at[:, pl.ds(j * CW, CW)], wo4.at[j, my_wo, :], ld.at[9]).start()
@@ -143,13 +144,16 @@
     loads["tok"].wait()
     loads["gain"].wait()
     gain = gain_v[...].astype(F32).reshape(1, D)
-    for q in range(4):
-        part = tok[q * QUARTER:(q + 1) * QUARTER, :].astype(F32)
-        mean = jnp.mean(part * part, axis=-1, keepdims=True)
-        xg[pl.ds(mult(base + q * QUARTER, QUARTER), QUARTER), :] = (
-            part * lax.rsqrt(mean + EPS) * gain
-        ).astype(BF16)
-
+
+    def normalise(*quarters):
+        for q in quarters:
+            part = tok[q * QUARTER:(q + 1) * QUARTER, :].astype(F32)
+            mean = jnp.mean(part * part, axis=-1, keepdims=True)
+            xg[pl.ds(mult(base + q * QUARTER, QUARTER), QUARTER), :] = (
+                part * lax.rsqrt(mean + EPS) * gain
+            ).astype(BF16)
+
+    normalise(0, 2)
     pl.semaphore_wait(barrier, len(peers) + (z + NZ - 1) // NZ + (2 * NZ - 2 - z) // NZ)
     greet_round(0)
 
@@ -168,12 +172,12 @@
     def wait_piece(u, q):
         arrived(piece(u, q), agr.at[u * 4 + q])
 
-    def half_piece(u, q, side):
+    def part_piece(u, q, side):
         rows = pl.ds(mult(u * 128 + c * ROWS + q * QUARTER, QUARTER), QUARTER)
-        return xg.at[rows, side * (D // 2):(side + 1) * (D // 2)]
-
-    def relay_half(u, q, side, sem, device):
-        send(half_piece(u, q, side), half_piece(u, q, side), GATHER, sem, device)
+        return xg.at[rows, (D // 4 if side else 0):(D if side else D // 4)]
+
+    def relay_part(u, q, side, device):
+        send(part_piece(u, q, side), part_piece(u, q, side), GATHER, agr.at[u * 4 + q], device)
 
     def wait_sibling(u):
         arrived(xg.at[plane_rows(u, other_c), :], agd.at[u])
@@ -183,6 +187,8 @@
 
     own = unit(0, 0)
     for s in range(4):
+        if s == 1:
+            normalise(1, 3)
         if s < 3:
             relay(own, s, up)
             relay(own, (s + 2) % 4, down)
@@ -207,8 +213,8 @@
             send(wo_piece(j, slot), wo_piece(j, slot), WO, wor.at[j], far)
         send(wo_piece(j, slot), wo_piece(j, slot), WO_SIBLING, wod.at[CHUNKS], sibling)
 
-    def send_near_chunk(half):
-        part = wo4.at[NEAR_CHUNK, pl.ds(mult(slot * QCOLS + half * 128, 128), 128), :]
+    def send_near_chunk(first, rows):
+        part = wo4.at[NEAR_CHUNK, pl.ds(mult(slot * QCOLS + first, ROWS), rows), :]
         send(part, part, WO, wor.at[NEAR_CHUNK], pair)
 
     far_slot = other_x * 2 + c
@@ -305,7 +311,6 @@
 
     greeted_round(0)
     greet_round(1)
-    project(0, own)
     def relay_across(*quarters):
         for q in quarters:
             wait_piece(across, q)
@@ -315,7 +320,7 @@
     def relay_beside(q):
         for device, halved in ((up, 0), (down, 2)):
             if q == halved:
-                relay_half(beside, q, 0, agr.at[beside * 4 + q], device)
+                relay_part(beside, q, 0, device)
             else:
                 relay(beside, q, device)
 
@@ -331,8 +336,8 @@
         if s == 0:
             relay(own, 3, up)
             relay(own, 1, down)
-            relay_half(below, s, 1, agx.at[0], pair)
-            relay_half(above, r, 1, agx.at[1], pair)
+            relay_part(below, s, 1, pair)
+            relay_part(above, r, 1, pair)
         wait_piece(beside, s)
         for q in ((), (0, 1), (2,), (3,))[s]:
             relay_beside(q)
@@ -343,12 +348,8 @@
     greet_round(2)
 
     def wait_x_neighbours(q):
-        for k, (u, halved) in enumerate(((x_below, 0), (x_above, 2))):
-            if q == halved:
-                arrived(half_piece(u, q, 0), agr.at[u * 4 + q])
-                arrived(half_piece(u, q, 1), agx.at[k])
-            else:
-                wait_piece(u, q)
+        for u in (x_below, x_above):
+            wait_piece(u, q)
             relay_sibling(u, q)
 
     def wait_x_across(*quarters):
@@ -356,9 +357,9 @@
             wait_piece(x_across, q)
             relay_sibling(x_across, q)
 
+    relay_across(1, 3)
+    project(0, own)
     project(1, below)
-    relay_across(1, 3)
-    send_near_chunk(0)
     project(2, above)
     forward_wo(0)
     project(3, beside)
@@ -374,7 +375,7 @@
     make_pairs([5], [x_across])
     wait_x_neighbours(3)
     make_pairs([6, 7], [x_below, x_above])
-    send_near_chunk(1)
+    send_near_chunk(0, 192)
 
     made_here = [
         jnp.logical_and(y == 0, x == 0),
@@ -493,11 +494,40 @@
     attend(0)
     forward_wo(4)
     attend(1)
+    send_near_chunk(192, 64)
     forward_wo(5)
     attend(2)
-    forward_wo(NEAR_CHUNK)
     attend(3)
-
+    gathered(0)
+
+    far_rows, up_rows, down_rows, own_rows = (slice(k * ROWS, (k + 1) * ROWS) for k in range(4))
+    arrived(wo4.at[:, pl.ds(mult(sibling_slot * QCOLS, QCOLS), QCOLS), :], wod.at[CHUNKS])
+
+    def far_target(j):
+        arrived(wo_piece(j, far_sibling_slot), wod.at[j])
+        product = jnp.dot(ctx4[far_rows, :], wo4[j], preferred_element_type=F32)
+        pbuf[j, far_rows, :] = product.astype(BF16)
+        send(pbuf.at[j, far_rows, :], ra.at[j], SUM, rar.at[j], down if j % 2 else up)
+
+    def near_targets(j):
+        product = jnp.dot(ctx4[ROWS:256, :], wo4[j], preferred_element_type=F32)
+        pbuf[j, ROWS:256, :] = product.astype(BF16)
+        if j % 2 == 0:
+            send(pbuf.at[j, down_rows, :], rfa.at[j], SUM, rbr.at[j], down)
+        else:
+            send(pbuf.at[j, up_rows, :], rfb.at[j], SUM, rbr.at[j], up)
+
+    def relay_sum(j):
+        rows = up_rows if j % 2 == 0 else down_rows
+        arrived(ra.at[j], rar.at[j])
+        pbuf[j, rows, :] = (pbuf[j, rows, :].astype(F32) + ra[j].astype(F32)).astype(BF16)
+        if j % 2 == 0:
+            send(pbuf.at[j, rows, :], rfb.at[j], SUM, rbr.at[j], up)
+        else:
+            send(pbuf.at[j, rows, :], rfa.at[j], SUM, rbr.at[j], down)
+
+    for j in range(2):
+        far_target(j)
     loads["weights"].wait()
     summary = jnp.dot(split3(weights_v[...]), ctx[...], preferred_element_type=F32)
     summary = split3(jnp.sum(summary, axis=0, keepdims=True))
@@ -505,54 +535,24 @@
         term = jnp.dot(summary, wo4[j, my_cols, :], preferred_element_type=F32)
         cy[y, j:j + 1, :] = jnp.sum(term, axis=0, keepdims=True)
     stage_start(0)
-    gathered(0)
-
-    far_rows, up_rows, down_rows, own_rows = (slice(k * ROWS, (k + 1) * ROWS) for k in range(4))
-    arrived(wo4.at[:, pl.ds(mult(sibling_slot * QCOLS, QCOLS), QCOLS), :], wod.at[CHUNKS])
-
-    def far_target(j):
-        arrived(wo_piece(j, far_sibling_slot), wod.at[j])
-        product = jnp.dot(ctx4[far_rows, :], wo4[j], preferred_element_type=F32)
-        pbuf[j, far_rows, :] = product.astype(BF16)
-        send(pbuf.at[j, far_rows, :], ra.at[j], SUM, rar.at[j], down if j % 2 else up)
-
-    def near_targets(j):
-        product = jnp.dot(ctx4[ROWS:256, :], wo4[j], preferred_element_type=F32)
-        pbuf[j, ROWS:256, :] = product.astype(BF16)
-        if j % 2 == 0:
-            send(pbuf.at[j, down_rows, :], rfa.at[j], SUM, rtr.at[j], down)
-        else:
-            send(pbuf.at[j, up_rows, :], rfb.at[j], SUM, rbr.at[j], up)
-
-    def relay_sum(j):
-        rows = up_rows if j % 2 == 0 else down_rows
-        arrived(ra.at[j], rar.at[j])
-        pbuf[j, rows, :] = (pbuf[j, rows, :].astype(F32) + ra[j].astype(F32)).astype(BF16)
-        if j % 2 == 0:
-            send(pbuf.at[j, rows, :], rfb.at[j], SUM, rbr.at[j], up)
-        else:
-            send(pbuf.at[j, rows, :], rfa.at[j], SUM, rtr.at[j], down)
-
-    early = [j for j in range(CHUNKS) if j != LAST_CHUNK]
-    for j in early:
+    for j in range(2, 6):
         far_target(j)
-    forward_wo(LAST_CHUNK)
+    forward_wo(7)
+    forward_wo(6)
+    far_target(7)
+    far_target(6)
+    stage_end(0)
+    stage_start(1)
     for k in range(1, 4):
         gathered(k)
-    for j in early:
+    for j in range(CHUNKS):
         near_targets(j)
-        if j == 1:
-            stage_end(0)
-            stage_start(1)
-    far_target(LAST_CHUNK)
-    near_targets(LAST_CHUNK)
-    for j in early + [LAST_CHUNK]:
+    for j in range(CHUNKS):
         relay_sum(j)
     stage_end(1)
     stage_start(2)
-    for j in early + [LAST_CHUNK]:
-        arrived(rfb.at[j], rbr.at[j])
-        arrived(rfa.at[j], rtr.at[j])
+    for j in range(CHUNKS):
+        arrived(pbuf.at[j, 0:2 * ROWS, :], rbr.at[j])
         total = pbuf[j, own_rows, :].astype(F32) + rfb[j].astype(F32) + rfa[j].astype(F32)
         cols = slice(j * CW, (j + 1) * CW)
         out[:, cols] = total.astype(BF16)
@@ -636,8 +636,8 @@
             vmem((NY, CHUNKS, CW), F32),
             vmem((NZ, CHUNKS, CW), F32),
             vmem((8, CHUNKS, CW), F32),
-            dma((10,)), dma((32,)), dma((2,)), dma((8,)), dma((2,)), dma((CHUNKS,)), dma((CHUNKS + 1,)),
-            dma((4,)), dma, dma((4,)), dma((CHUNKS,)), dma((CHUNKS,)), dma((CHUNKS,)),
+            dma((10,)), dma((32,)), dma((8,)), dma((2,)), dma((CHUNKS,)), dma((CHUNKS + 1,)),
+            dma((4,)), dma, dma((4,)), dma((CHUNKS,)), dma((CHUNKS,)),
             dma((3,)), dma((12,)), pltpu.SemaphoreType.REGULAR((6,)),
         ],
         compiler_params=pltpu.CompilerParams(

time: 69.1 us -> 68.7 us (level)
  no operation moved by 1% of the time
where the time goes in v5:
time: 68.7 us; the launch traced here: 68.6 us
  Pallas kernels  67.8 us (99%)
  between operations  0.82 us (1%)
    pallas_call x1, Pallas kernels, local(): pl.pallas_call(kernel, out_shape=(pltpu.VMEM((ROWS, D), BF16), pltpu.VMEM...  67 us

profile of v5, /device:TPU:1, one launch (start us, length us, event | category | flops | bytes accessed | tf_op | source)
XLA Modules:
  0.0 68.6 jit_solution(10647958834564482510)
XLA Ops:
  0.6 67.0 %sublayer.1 = (bf16[64,4096]{1,0:T(8,128)(2,1)S(1)}, f32[1,4096]{1,0:T(1,128)S(1)}) custom-call(bf16[64,4096]{1,0:T(8,128)(2,1)} %bitcast.4, bf16[4096]{0:T(1024)(128)(2,1)} %gain_in.1, bf16[256]{0:T(256)(128)(2,1)} %bq_in.1, bf16[64]{0:T(256)(128)(2,1)} %bkv_in.1, bf16[4096,256]{1,0:T(8,128)(2,1)} %wq.1, bf16[64,4096]{1,0:T(8,128)(2,1)} %bitcast.5, ...), custom_call_target="tpu_custom_call" | custom-call | tf_op jit(solution)/shard_map/sublayer/pallas_call | solution.py:604
  67.6 0.8 %store_results.1 = (bf16[64,4096]{1,0:T(8,128)(2,1)}, f32[1,4096]{1,0:T(1,128)}) custom-call(bf16[64,4096]{1,0:T(8,128)(2,1)S(1)} %get-tuple-element.6.attended, f32[1,4096]{1,0:T(1,128)S(1)} %get-tuple-element.7.total), custom_call_target="tpu_custom_call" | custom-call | tf_op jit(solution)/shard_map/store_results/pallas_call | solution.py:648

commit v6 on v5

--- a/solution.py
+++ b/solution.py
@@ -417,44 +417,51 @@
     def theirs(dx, dc):
         return ((x + dx) % 2) * 2 + (c + dc) % 2
 
-    def head_attention(v, h):
+    def attention(v, start, count):
         block, before = slice(v * 256, (v + 1) * 256), slice(0, v * 256)
-        row = lax.broadcasted_iota(jnp.int32, (256, 256), 0)
-        col = lax.broadcasted_iota(jnp.int32, (256, 256), 1)
-        cols = slice(h * HD, (h + 1) * HD)
-        query = qb[block, cols]
-        diagonal = lax.dot_general(query, kv[0, block, :], contract_last, preferred_element_type=F32)
-        diagonal = jnp.where(row >= col, diagonal, -1e30)
-        top = jnp.max(diagonal, axis=-1, keepdims=True)
-        if v:
-            earlier = lax.dot_general(query, kv[0, before, :], contract_last, preferred_element_type=F32)
-            top = jnp.maximum(top, jnp.max(earlier, axis=-1, keepdims=True))
-        weight = jnp.exp((diagonal - top) * scale)
-        total = jnp.sum(weight, axis=-1, keepdims=True)
-        mixed = jnp.dot(weight.astype(BF16), kv[1, block, :], preferred_element_type=F32)
-        if v:
-            weight = jnp.exp((earlier - top) * scale)
-            total += jnp.sum(weight, axis=-1, keepdims=True)
-            mixed += jnp.dot(weight.astype(BF16), kv[1, before, :], preferred_element_type=F32)
-        ctx[block, cols] = (mixed / total).astype(BF16)
+        rows = pl.ds(mult(v * 256 + start, 128), count)
+        row = lax.broadcasted_iota(jnp.int32, (count, 256), 0) + start
+        col = lax.broadcasted_iota(jnp.int32, (count, 256), 1)
+        for h in range(2):
+            cols = slice(h * HD, (h + 1) * HD)
+            query = qb[rows, cols]
+            diagonal = lax.dot_general(query, kv[0, block, :], contract_last, preferred_element_type=F32)
+            diagonal = jnp.where(row >= col, diagonal, -1e30)
+            top = jnp.max(diagonal, axis=-1, keepdims=True)
+            if v:
+                earlier = lax.dot_general(query, kv[0, before, :], contract_last, preferred_element_type=F32)
+                top = jnp.maximum(top, jnp.max(earlier, axis=-1, keepdims=True))
+            weight = jnp.exp((diagonal - top) * scale)
+            total = jnp.sum(weight, axis=-1, keepdims=True)
+            mixed = jnp.dot(weight.astype(BF16), kv[1, block, :], preferred_element_type=F32)
+            if v:
+                weight = jnp.exp((earlier - top) * scale)
+                total += jnp.sum(weight, axis=-1, keepdims=True)
+                mixed += jnp.dot(weight.astype(BF16), kv[1, before, :], preferred_element_type=F32)
+            ctx[rows, cols] = (mixed / total).astype(BF16)
 
     def attend(k):
         b = (y + (2, 1, 3, 0)[k]) % NY
         target = pl.ds(k * ROWS, ROWS)
-        for h in range(2):
+
+        def part(start, count, users):
             for v in range(NY):
                 @pl.when(b == v)
-                def _(v=v, h=h):
-                    head_attention(v, h)
-
-            cols = slice(h * HD, (h + 1) * HD)
-            head = pl.ds(mult(slot * QCOLS + h * HD, HD), HD)
-            for dx, dc in beyond:
+                def _(v=v):
+                    attention(v, start, count)
+
+            for dx, dc in users:
                 send(
-                    ctx.at[pl.ds(mult(b * 256 + theirs(dx, dc) * ROWS, ROWS), ROWS), cols],
-                    ctx4.at[target, head],
+                    ctx.at[pl.ds(mult(b * 256 + theirs(dx, dc) * ROWS, ROWS), ROWS), :],
+                    ctx4.at[target, my_cols],
                     CONTEXT, cxr.at[k], at(dx=dx, dc=dc),
                 )
+
+        if k == 0:
+            part(other_x * 128, 128, beyond[:2])
+            part(x * 128, 128, beyond[2:])
+        else:
+            part(0, 256, beyond)
         ctx4[target, my_cols] = ctx[pl.ds(mult(b * 256 + slot * ROWS, ROWS), ROWS), :]
 
     def gathered(k):
@@ -539,13 +546,15 @@
         far_target(j)
     forward_wo(7)
     forward_wo(6)
-    far_target(7)
-    far_target(6)
     stage_end(0)
     stage_start(1)
     for k in range(1, 4):
         gathered(k)
-    for j in range(CHUNKS):
+    for j in range(4):
+        near_targets(j)
+    far_target(7)
+    far_target(6)
+    for j in range(4, CHUNKS):
         near_targets(j)
     for j in range(CHUNKS):
         relay_sum(j)

time: 68.7 us -> 68.6 us (level); the launches traced: 68.6 us -> 67.7 us
  Pallas kernels: 67.8 us -> 66.8 us
    pallas_call x1, Pallas kernels: 67 us -> 66 us  [local(): pl.pallas_call(kernel, out_shape=(pltpu.VMEM((ROWS, D), BF16), pltpu.VMEM...]
where the time goes in v6:
time: 68.6 us; the launch traced here: 67.7 us
  Pallas kernels  66.8 us (97%)
  between operations  0.82 us (1%)
    pallas_call x1, Pallas kernels, local(): pl.pallas_call(kernel, out_shape=(pltpu.VMEM((ROWS, D), BF16), pltpu.VMEM...  66 us

profile of v6, /device:TPU:1, one launch (start us, length us, event | category | flops | bytes accessed | tf_op | source)
XLA Modules:
  0.0 67.7 jit_solution(9941566174809251438)
XLA Ops:
  0.6 66.0 %sublayer.1 = (bf16[64,4096]{1,0:T(8,128)(2,1)S(1)}, f32[1,4096]{1,0:T(1,128)S(1)}) custom-call(bf16[64,4096]{1,0:T(8,128)(2,1)} %bitcast.4, bf16[4096]{0:T(1024)(128)(2,1)} %gain_in.1, bf16[256]{0:T(256)(128)(2,1)} %bq_in.1, bf16[64]{0:T(256)(128)(2,1)} %bkv_in.1, bf16[4096,256]{1,0:T(8,128)(2,1)} %wq.1, bf16[64,4096]{1,0:T(8,128)(2,1)} %bitcast.5, ...), custom_call_target="tpu_custom_call" | custom-call | tf_op jit(solution)/shard_map/sublayer/pallas_call | solution.py:613
  66.7 0.8 %store_results.1 = (bf16[64,4096]{1,0:T(8,128)(2,1)}, f32[1,4096]{1,0:T(1,128)}) custom-call(bf16[64,4096]{1,0:T(8,128)(2,1)S(1)} %get-tuple-element.6.attended, f32[1,4096]{1,0:T(1,128)S(1)} %get-tuple-element.7.total), custom_call_target="tpu_custom_call" | custom-call | tf_op jit(solution)/shard_map/store_results/pallas_call | solution.py:657
